TPU v7x, 32 devices: a whole 2x2x4 slice. The times are simulated.
32 devices in a mesh: rep: 4 (over z), fsdp: 2 (over x), tp: 4 (over y, core).
Axes of the slice: x: 2, y: 2, z: 4, core: 2. Of those that a mesh axis runs over, the one named last changes fastest.
Arguments:
- gate_pre: bfloat16 [1024, 14848], P(('rep', 'fsdp'), 'tp'), may hold values from -6 to 6
- up_pre: bfloat16 [1024, 14848], P(('rep', 'fsdp'), 'tp'), may hold values from -30 to 30
- out_grad: bfloat16 [1024, 4096], P(('rep', 'fsdp')), may hold values from -30 to 30
Outputs:
- down_grad: bfloat16 [4096, 14848], P('fsdp', 'tp')
All inputs are finite; a program needn't handle non-finite values.
Results may differ from a plain program's by a relative error of at most 0.02.
Values may be sent and summed in bfloat16 or wider, within the bound.
A program may use at most 128 MiB of HBM per device.

v0:
```python
import functools

import jax
import jax.numpy as jnp
from jax import lax
from jax.experimental import pallas as pl
from jax.experimental.pallas import tpu as pltpu
from jax.sharding import PartitionSpec as P

MESH = pl.DeviceIdType.MESH
LANES = 128
VMEM_LIMIT = 60 * 1024 * 1024
WIDTH = 512
TILE = 512
LAG = 2
AHEAD = 2


class Chunk:
    def __init__(self, index, start, size):
        self.index, self.start, self.size = index, start, size

    @property
    def cols(self):
        start = self.start
        return pl.ds(start if isinstance(start, int) else pl.multiple_of(start, LANES), self.size)


def chunking(columns):
    head = columns % WIDTH
    first = 1 if head else 0
    count = first + columns // WIDTH

    def chunk(index):
        if isinstance(index, int) and index < first:
            return Chunk(index, 0, head)
        return Chunk(index, head + (index - first) * WIDTH, WIDTH)

    return first, count, chunk


def gather_multiply(
    entry_count, gate_ref, up_ref, grad_ref, out_ref, factor_ref,
    held, grads, turned, gate_in, up_in, sums, total_out,
    local_sem, gx_send, gx_recv, gz_recv, gz_out, gz_in, gy_send, gy_recv,
    gs_send, gs_recv, gf_send, gf_recv,
    z_recv, z_out, z_in, zo_recv, zo_send, x_send, x_recv,
    sq_send, sq_recv, fa_send, fa_recv,
):
    rep = lax.axis_index("rep")
    fsdp = lax.axis_index("fsdp")
    tp = lax.axis_index("tp")
    rows, columns = gate_ref.shape
    half = grads.shape[1]
    n_tp = 4
    quarter = half // n_tp
    first, count, chunk = chunking(columns)
    other = 1 - fsdp
    side = rep // 2
    edge, near, far, far_edge = 3 * side, 1 + side, 2 - side, 3 - 3 * side
    is_edge = rep == edge
    inner = jnp.where(is_edge, near, far)
    sibling = tp + 1 - 2 * lax.rem(tp, 2)
    opposite = lax.rem(tp + 2, n_tp)
    past = lax.rem(sibling + 2, n_tp)

    def rows_of(r, s):
        return pl.ds(pl.multiple_of((r * 2 + s) * rows, rows), rows)

    def quarter_of(t):
        return pl.ds(pl.multiple_of(t * quarter, LANES), quarter)

    def remote(src, dst, send, recv, device):
        return pltpu.make_async_remote_copy(
            src_ref=src, dst_ref=dst, send_sem=send, recv_sem=recv,
            device_id=device, device_id_type=MESH,
        )

    loads = [
        pltpu.make_async_copy(gate_ref, gate_in, local_sem.at[0]),
        pltpu.make_async_copy(up_ref, up_in, local_sem.at[1]),
        pltpu.make_async_copy(
            grad_ref.at[:, pl.ds(pl.multiple_of(fsdp * half, LANES), half)],
            grads.at[rows_of(rep, fsdp), :], local_sem.at[2],
        ),
    ]
    for load in loads:
        load.start()

    barrier = pltpu.get_barrier_semaphore()
    for k in range(n_tp):
        if k:
            pl.semaphore_signal(
                barrier, inc=1, device_id={"tp": lax.rem(tp + k, n_tp)}, device_id_type=MESH
            )
        pl.semaphore_signal(
            barrier, inc=1, device_id={"fsdp": other, "tp": lax.rem(tp + k, n_tp)},
            device_id_type=MESH,
        )
    pl.semaphore_signal(barrier, inc=1, device_id={"rep": inner}, device_id_type=MESH)

    @pl.when(jnp.logical_not(is_edge))
    def _():
        pl.semaphore_signal(barrier, inc=1, device_id={"rep": edge}, device_id_type=MESH)

    pl.semaphore_wait(barrier, 2 * n_tp + jnp.where(is_edge, 0, 1))

    def grad_across():
        src = grad_ref.at[:, pl.ds(pl.multiple_of(other * half + tp * quarter, LANES), quarter)]
        return remote(src, grads.at[rows_of(rep, fsdp), quarter_of(tp)], gx_send, gx_recv, {"fsdp": other})

    def grad_spot(r, s, t):
        return grads.at[rows_of(r, s), quarter_of(t)]

    def grad_hop(r, s, own, inward):
        spot = grad_spot(r, s, tp)
        src = spot
        if own:
            src = grad_ref.at[:, pl.ds(pl.multiple_of(fsdp * half + tp * quarter, LANES), quarter)]
        to = inner if inward else edge
        return remote(src, spot, (gz_in if inward else gz_out).at[r, s], gz_recv.at[r, s], {"rep": to})

    def grad_got(r, s):
        spot = grad_spot(r, s, tp)
        return remote(spot, spot, gz_in.at[r, s], gz_recv.at[r, s], {"rep": inner})

    def over_y(r, s, t):
        spot = grad_spot(r, s, t)
        return remote(spot, spot, gy_send.at[r, s], gy_recv.at[r, s], {"tp": opposite})

    def to_sibling(r, s, t):
        spot = grad_spot(r, s, t)
        return remote(spot, spot, gs_send.at[r, s], gs_recv.at[r, s], {"tp": sibling})

    def pass_sibling(r, s, t):
        spot = grad_spot(r, s, t)
        return remote(spot, spot, gf_send.at[r, s], gf_recv.at[r, s], {"tp": sibling})

    def hop(r, ch, inward):
        spot = held.at[rows_of(r, fsdp), ch.cols]
        to = inner if inward else edge
        return remote(spot, spot, (z_in if inward else z_out).at[r, ch.index], z_recv.at[r, ch.index], {"rep": to})

    def hop_got(r, ch):
        spot = held.at[rows_of(r, fsdp), ch.cols]
        return remote(spot, spot, z_in.at[r, ch.index], z_recv.at[r, ch.index], {"rep": inner})

    def hop_other(ch):
        spot = held.at[rows_of(edge, other), ch.cols]
        return remote(spot, spot, zo_send.at[ch.index], zo_recv.at[ch.index], {"rep": inner})

    def cross(r, ch):
        spot = held.at[rows_of(r, fsdp), ch.cols]
        return remote(spot, spot, x_send.at[r, ch.index], x_recv.at[r, ch.index], {"fsdp": other})

    def crossed(r, ch):
        spot = held.at[rows_of(r, other), ch.cols]
        return remote(spot, spot, x_send.at[r, ch.index], x_recv.at[r, ch.index], {"fsdp": other})

    def on_edge(act):
        pl.when(is_edge)(act)

    def on_middle(act):
        pl.when(jnp.logical_not(is_edge))(act)

    def chunks_from(low, high, act):
        while low < high and low < first:
            act(chunk(low))
            low += 1
        if low < high:
            @pl.loop(low, high)
            def _(index):
                act(chunk(index))

    grad_across().start()
    grad_hop(rep, fsdp, True, True).start()
    on_middle(lambda: grad_hop(rep, fsdp, True, False).start())

    loads[0].wait()
    loads[1].wait()

    @pl.loop(0, columns // LANES)
    def _(at):
        cols = pl.ds(pl.multiple_of(at * LANES, LANES), LANES)
        gate = gate_in[:, cols].astype(jnp.float32)
        held[rows_of(rep, fsdp), cols] = (
            jax.nn.silu(gate) * up_in[:, cols].astype(jnp.float32)
        ).astype(held.dtype)

    chunks_from(0, count, lambda ch: cross(rep, ch).start())
    hop(rep, chunk(0), True).start()
    on_middle(lambda: hop(rep, chunk(0), False).start())

    def share(r, s):
        over_y(r, s, tp).start()
        to_sibling(r, s, tp).start()

    def pass_on(r, s):
        over_y(r, s, opposite).wait_recv()
        pass_sibling(r, s, opposite).start()

    def settle(r, s):
        to_sibling(r, s, sibling).wait_recv()
        pass_sibling(r, s, past).wait_recv()

    tile = 256

    def turn(r):
        spot = pl.ds(pl.multiple_of(r * 2 * rows, 2 * rows), 2 * rows)

        @pl.loop(0, half // tile)
        def _(m):
            part = pl.ds(pl.multiple_of(m * tile, tile), tile)
            turned[part, spot] = grads[spot, part].T

    def take_own():
        grad_across().wait_recv()
        grad_hop(rep, other, False, True).start()
        on_middle(lambda: grad_hop(rep, other, False, False).start())
        share(rep, other)

    def spread(items, take, after):
        waiting = {}

        def land(name, r, s):
            pass_on(r, s)
            waiting.setdefault(name, []).append((r, s))
            if len(waiting[name]) == (1 if name == "own" else 2):
                for pair in waiting[name]:
                    settle(*pair)
                turn(r)

        for at, item in enumerate(items):
            take(*item)
            after(at)
            if at:
                land(*items[at - 1])
        land(*items[-1])

    loads[2].wait()

    @on_edge
    def _():
        share_of = [(at * count // 7, (at + 1) * count // 7) for at in range(7)]

        def take(name, r, s):
            if name == "own":
                take_own()
                chunks_from(1, count, lambda ch: hop(rep, ch, True).start())
            else:
                grad_got(r, s).wait_recv()
                share(r, s)

        def after(at):
            def act(ch):
                crossed(edge, ch).wait_recv()
                hop_other(ch).start()
            chunks_from(*share_of[at], act)

        spread(
            [("own", rep, other), ("near", near, fsdp), ("near", near, other),
             ("far", far, fsdp), ("far", far, other),
             ("last", far_edge, fsdp), ("last", far_edge, other)],
            take, after,
        )

    @on_middle
    def _():
        def take(name, r, s):
            if name == "own":
                take_own()
                return
            grad_got(r, s).wait_recv()
            grad_hop(r, s, False, name == "edge").start()
            share(r, s)

        spread(
            [("own", rep, other), ("edge", edge, fsdp), ("far", far, fsdp),
             ("edge", edge, other), ("far", far, other),
             ("last", far_edge, fsdp), ("last", far_edge, other)],
            take, lambda at: None,
        )

    def clear():
        sums[fsdp * n_tp + tp] = jnp.zeros(sums.shape[1:], sums.dtype)

    def multiply_tile(ch, m, squared):
        spot = pl.ds(pl.multiple_of(m * TILE, TILE), TILE)
        product = jnp.dot(turned[spot, :], held[:, ch.cols], preferred_element_type=jnp.float32)
        out_ref[spot, ch.cols] = product.astype(out_ref.dtype)
        if squared:
            squares = jnp.sum((product * product).reshape(TILE // 8, 8, ch.size), axis=0)
            total = squares[:, :LANES]
            for at in range(LANES, ch.size, LANES):
                total = total + squares[:, at:at + LANES]
            sums[fsdp * n_tp + tp] += total

    tiles = half // TILE

    def sweep(events, arrived, squared):
        places = [at * tiles // len(events) for at in range(len(events))]

        def step(index, lagging):
            def at_tile(m):
                for place, event in zip(places, events):
                    pl.when(m == place)(lambda: event(chunk(index)))
                if lagging is not None:
                    multiply_tile(lagging, m, squared)
            if lagging is not None:
                arrived(lagging)
                pl.loop(0, tiles)(at_tile)
            else:
                for event in events:
                    event(chunk(index))

        start = min(count, first + LAG)
        for index in range(start):
            step(index, chunk(index - LAG) if index >= LAG else None)

        @pl.loop(start, count)
        def _(index):
            step(index, chunk(index - LAG))

        def finish(ch):
            arrived(ch)
            pl.loop(0, tiles)(lambda m: multiply_tile(ch, m, squared))
        chunks_from(max(count - LAG, 0), count, finish)

    @on_edge
    def _():
        def pull(r):
            def event(ch):
                hop_got(r, ch).wait_recv()
                cross(r, ch).start()
            return event

        def arrived(ch):
            for r in (near, far, far_edge):
                crossed(r, ch).wait_recv()

        sweep([pull(near), pull(far), pull(far_edge)], arrived, False)

    @on_middle
    def _():
        def inward(ch):
            hop(rep, ch, True).start()
            hop_got(edge, ch).wait_recv()
            hop(edge, ch, True).start()

        hop_got(edge, chunk(0)).wait_recv()
        hop(edge, chunk(0), True).start()
        chunks_from(1, min(1 + AHEAD, count), inward)

        def outer(ch):
            index = ch.index
            if isinstance(index, int):
                if index:
                    hop(rep, ch, False).start()
                    if index + AHEAD < count:
                        inward(chunk(index + AHEAD))
            else:
                hop(rep, ch, False).start()
                pl.when(index + AHEAD < count)(lambda: inward(chunk(index + AHEAD)))

        def pull(r):
            def event(ch):
                hop_got(r, ch).wait_recv()
                hop(r, ch, False).start()
                cross(r, ch).start()
            return event

        def arrived(ch):
            hop_other(ch).wait_recv()
            for r in (rep, far, far_edge):
                crossed(r, ch).wait_recv()

        clear()
        sweep([outer, pull(far), pull(far_edge)], arrived, True)

        mine = fsdp * n_tp + tp
        peers = [(a, k) for a in range(2) for k in range(n_tp) if a or k]

        def exchange(at, towards):
            a, k = peers[at]
            to_side = other if a else fsdp
            to_tp = lax.rem(tp + (k if towards else n_tp - k), n_tp)
            spot = sums.at[mine if towards else to_side * n_tp + to_tp]
            return remote(spot, spot, sq_send.at[at], sq_recv.at[at], {"fsdp": to_side, "tp": to_tp})

        for at in range(len(peers)):
            exchange(at, True).start()
        for at in range(len(peers)):
            exchange(at, False).wait_recv()
        square_total = jnp.sum(jnp.sum(sums[...], axis=0), keepdims=True)
        factor = 1.0 / jnp.sqrt(square_total / entry_count + 1e-06)
        total_out[...] = jnp.broadcast_to(factor, total_out.shape)
        for at in range(len(peers)):
            exchange(at, True).wait_send()

    def tell():
        return remote(total_out, total_out, fa_send, fa_recv, {"rep": jnp.where(is_edge, near, edge)})

    on_middle(lambda: tell().start())
    on_edge(lambda: tell().wait_recv())
    factor_ref[...] = total_out[...]

    grad_across().wait_send()

    def sent_shares(r, s):
        over_y(r, s, tp).wait_send()
        to_sibling(r, s, tp).wait_send()
        pass_sibling(r, s, opposite).wait_send()

    sent_shares(rep, other)
    grad_hop(rep, fsdp, True, True).wait_send()
    grad_hop(rep, other, False, True).wait_send()
    chunks_from(0, count, lambda ch: cross(rep, ch).wait_send())

    @on_edge
    def _():
        for r in (near, far, far_edge):
            for s in (fsdp, other):
                sent_shares(r, s)

        def sent(ch):
            hop(rep, ch, True).wait_send()
            hop_other(ch).wait_send()
            for r in (near, far, far_edge):
                cross(r, ch).wait_send()
        chunks_from(0, count, sent)

    @on_middle
    def _():
        tell().wait_send()
        for s, own in ((fsdp, True), (other, False)):
            grad_hop(rep, s, own, False).wait_send()
            grad_hop(edge, s, False, True).wait_send()
            for r in (edge, far, far_edge):
                sent_shares(r, s)
            for r in (far, far_edge):
                grad_hop(r, s, False, False).wait_send()

        def sent(ch):
            for r in (rep, edge):
                hop(r, ch, True).wait_send()
            for r in (rep, far, far_edge):
                hop(r, ch, False).wait_send()
            for r in (far, far_edge):
                cross(r, ch).wait_send()
        chunks_from(0, count, sent)


def by_kernel(n_rep, n_tp, entry_count, gate_pre, up_pre, out_grad):
    rows, columns = gate_pre.shape
    tokens = rows * n_rep * 2
    half = out_grad.shape[1] // 2
    count = chunking(columns)[1]
    dma = pltpu.SemaphoreType.DMA
    block, piece = dma((n_rep, 2)), dma((n_rep, count))
    return pl.pallas_call(
        functools.partial(gather_multiply, entry_count),
        out_shape=(
            pltpu.VMEM((half, columns), jnp.bfloat16),
            pltpu.VMEM((8, LANES), jnp.float32),
        ),
        in_specs=[pl.BlockSpec(memory_space=pl.ANY)] * 3,
        out_specs=(pl.BlockSpec(memory_space=pltpu.VMEM), pl.BlockSpec(memory_space=pltpu.VMEM)),
        scratch_shapes=[
            pltpu.VMEM((tokens, columns), jnp.bfloat16),
            pltpu.VMEM((tokens, half), jnp.bfloat16),
            pltpu.VMEM((half, tokens), jnp.bfloat16),
            pltpu.VMEM((rows, columns), jnp.bfloat16),
            pltpu.VMEM((rows, columns), jnp.bfloat16),
            pltpu.VMEM((2 * n_tp, 8, LANES), jnp.float32),
            pltpu.VMEM((8, LANES), jnp.float32),
            dma((3,)), dma, dma, block, block, block, block, block,
            block, block, block, block,
            piece, piece, piece, dma((count,)), dma((count,)), piece, piece,
            dma((2 * n_tp - 1,)), dma((2 * n_tp - 1,)), dma, dma,
        ],
        compiler_params=pltpu.CompilerParams(
            collective_id=0, has_side_effects=True, vmem_limit_bytes=VMEM_LIMIT * 3 // 4
        ),
    )(gate_pre, up_pre, out_grad)


def scale(summed, factors):
    half, columns = summed.shape
    rows = 128

    def body(summed_ref, factor_ref, out_ref, ready, sems):
        steps = half // rows
        depth = ready.shape[0]

        def leave(m):
            slot = lax.rem(m, depth)
            spot = pl.ds(pl.multiple_of(m * rows, rows), rows)
            return pltpu.make_async_copy(ready.at[slot], out_ref.at[spot, :], sems.at[slot])

        @pl.loop(0, steps)
        def _(m):
            slot = lax.rem(m, depth)
            spot = pl.ds(pl.multiple_of(m * rows, rows), rows)

            @pl.when(m >= depth)
            def _():
                leave(m - depth).wait()
            for at in range(0, columns, LANES):
                cols = pl.ds(at, LANES)
                scaled = summed_ref[spot, cols].astype(jnp.float32) * factor_ref[0:1, :]
                ready[slot, :, cols] = scaled.astype(ready.dtype)
            leave(m).start()

        @pl.loop(max(steps - depth, 0), steps)
        def _(m):
            leave(m).wait()

    return pl.pallas_call(
        body,
        out_shape=jax.ShapeDtypeStruct((half, columns), jnp.bfloat16),
        in_specs=[pl.BlockSpec(memory_space=pltpu.VMEM)] * 2,
        out_specs=pl.BlockSpec(memory_space=pl.ANY),
        scratch_shapes=[pltpu.VMEM((4, rows, columns), jnp.bfloat16), pltpu.SemaphoreType.DMA((4,))],
        compiler_params=pltpu.CompilerParams(vmem_limit_bytes=16 * 1024 * 1024),
    )(summed, factors)


def by_xla(gate_pre, up_pre, out_grad):
    hidden = (jax.nn.silu(gate_pre.astype(jnp.float32)) * up_pre.astype(jnp.float32)).astype(
        jnp.bfloat16
    )
    spread = lax.all_to_all(out_grad, "fsdp", split_axis=1, concat_axis=0, tiled=True)
    grad_rows = lax.all_gather(spread, "rep", axis=0, tiled=True)
    hidden_rows = lax.all_gather(hidden, ("rep", "fsdp"), axis=0, tiled=True)
    summed = lax.dot_general(
        grad_rows, hidden_rows, (((0,), (0,)), ((), ())), preferred_element_type=jnp.float32
    )
    return summed, jnp.sum(summed * summed)


def kernel_fits(n_rep, n_fsdp, n_tp, rows, columns, features):
    tokens, half = rows * n_rep * n_fsdp, features // n_fsdp
    held_bytes = 2 * (tokens * columns + 2 * tokens * half + half * columns + 2 * rows * columns)
    aligned = rows % 128 == 0 and columns % LANES == 0 and half % (LANES * n_tp) == 0
    shaped = (n_rep, n_fsdp, n_tp) == (4, 2, 4) and columns >= 4 * WIDTH
    return shaped and aligned and half % TILE == 0 and held_bytes < VMEM_LIMIT * 3 // 4


def solution(mesh):
    n_rep, n_fsdp, n_tp = (mesh.shape[axis] for axis in ("rep", "fsdp", "tp"))

    def on_device(gate_pre, up_pre, out_grad):
        half, columns = out_grad.shape[1] // n_fsdp, gate_pre.shape[1]
        entry_count = half * n_fsdp * columns * n_tp
        if kernel_fits(n_rep, n_fsdp, n_tp, *gate_pre.shape, out_grad.shape[1]):
            summed, factors = by_kernel(n_rep, n_tp, entry_count, gate_pre, up_pre, out_grad)
            return scale(summed, factors)
        summed, square_sum = by_xla(gate_pre, up_pre, out_grad)
        square_total = lax.psum(square_sum, ("fsdp", "tp"))
        factor = 1.0 / jnp.sqrt(square_total / entry_count + 1e-06)
        return (summed * factor).astype(jnp.bfloat16)

    return jax.shard_map(
        on_device,
        mesh=mesh,
        in_specs=(P(("rep", "fsdp"), "tp"), P(("rep", "fsdp"), "tp"), P(("rep", "fsdp"), None)),
        out_specs=P("fsdp", "tp"),
        check_vma=False,
    )
```

profile of v0, /device:TPU:0, one launch (start us, length us, event | category | flops | bytes accessed | tf_op | source)
XLA Modules:
  0.0 115.4 jit_solution(863019104656422346)
XLA Ops:
  0.0 109.8 %shard_map.37 = (bf16[2048,3712]{1,0:T(8,128)(2,1)S(1)}, f32[8,128]{1,0:T(8,128)S(1)}) custom-call(bf16[128,3712]{1,0:T(8,128)(2,1)} %gate_ref.1, bf16[128,3712]{1,0:T(8,128)(2,1)} %up_ref.1, bf16[128,4096]{1,0:T(8,128)(2,1)} %grad_ref.1), custom_call_target="tpu_custom_call" | custom-call | tf_op jit(solution)/shard_map/pallas_call | solution.py:460
  109.9 5.6 %shard_map.38 = bf16[2048,3712]{1,0:T(8,128)(2,1)} custom-call(bf16[2048,3712]{1,0:T(8,128)(2,1)S(1)} %get-tuple-element.7.summed_ref, f32[8,128]{1,0:T(8,128)S(1)} %get-tuple-element.8.factor_ref), custom_call_target="tpu_custom_call" | custom-call | tf_op jit(solution)/shard_map/pallas_call | solution.py:518
where the time goes:
time: 116 us; the launch traced here: 115 us
  Pallas kernels  115 us (99%)
    pallas_call x1, Pallas kernels, by_kernel(): pl.pallas_call(functools.partial(gather_multiply, entry_count), out_shape...  110 us
    pallas_call x1, Pallas kernels, scale(): pl.pallas_call(body, out_shape=jax.ShapeDtypeStruct((half, columns), jnp....  5.58 us

commit v1 on v0

--- a/solution.py
+++ b/solution.py
@@ -10,10 +10,10 @@
 MESH = pl.DeviceIdType.MESH
 LANES = 128
 VMEM_LIMIT = 60 * 1024 * 1024
-WIDTH = 512
-TILE = 512
-LAG = 2
-AHEAD = 2
+WIDTH = 256
+TILE = 1024
+LAG = 4
+AHEAD = 4
 
 
 class Chunk:
@@ -103,7 +103,20 @@
     def _():
         pl.semaphore_signal(barrier, inc=1, device_id={"rep": edge}, device_id_type=MESH)
 
-    pl.semaphore_wait(barrier, 2 * n_tp + jnp.where(is_edge, 0, 1))
+    with jax.named_scope("load"):
+        loads[0].wait()
+        loads[1].wait()
+
+    @pl.loop(0, columns // LANES)
+    def _(at):
+        cols = pl.ds(pl.multiple_of(at * LANES, LANES), LANES)
+        gate = gate_in[:, cols].astype(jnp.float32)
+        held[rows_of(rep, fsdp), cols] = (
+            jax.nn.silu(gate) * up_in[:, cols].astype(jnp.float32)
+        ).astype(held.dtype)
+
+    with jax.named_scope("barrier"):
+        pl.semaphore_wait(barrier, 2 * n_tp + jnp.where(is_edge, 0, 1))
 
     def grad_across():
         src = grad_ref.at[:, pl.ds(pl.multiple_of(other * half + tp * quarter, LANES), quarter)]
@@ -176,20 +189,10 @@
     grad_hop(rep, fsdp, True, True).start()
     on_middle(lambda: grad_hop(rep, fsdp, True, False).start())
 
-    loads[0].wait()
-    loads[1].wait()
-
-    @pl.loop(0, columns // LANES)
-    def _(at):
-        cols = pl.ds(pl.multiple_of(at * LANES, LANES), LANES)
-        gate = gate_in[:, cols].astype(jnp.float32)
-        held[rows_of(rep, fsdp), cols] = (
-            jax.nn.silu(gate) * up_in[:, cols].astype(jnp.float32)
-        ).astype(held.dtype)
-
     chunks_from(0, count, lambda ch: cross(rep, ch).start())
-    hop(rep, chunk(0), True).start()
-    on_middle(lambda: hop(rep, chunk(0), False).start())
+    early = first + 1
+    chunks_from(0, early, lambda ch: hop(rep, ch, True).start())
+    on_middle(lambda: chunks_from(0, early, lambda ch: hop(rep, ch, False).start()))
 
     def share(r, s):
         over_y(r, s, tp).start()
@@ -219,67 +222,12 @@
         on_middle(lambda: grad_hop(rep, other, False, False).start())
         share(rep, other)
 
-    def spread(items, take, after):
-        waiting = {}
-
-        def land(name, r, s):
-            pass_on(r, s)
-            waiting.setdefault(name, []).append((r, s))
-            if len(waiting[name]) == (1 if name == "own" else 2):
-                for pair in waiting[name]:
-                    settle(*pair)
-                turn(r)
-
-        for at, item in enumerate(items):
-            take(*item)
-            after(at)
-            if at:
-                land(*items[at - 1])
-        land(*items[-1])
+    def perform(plan, acts):
+        for at, (name, *args) in enumerate(plan):
+            with jax.named_scope(f"{name}{at}"):
+                acts[name](*args)
 
     loads[2].wait()
-
-    @on_edge
-    def _():
-        share_of = [(at * count // 7, (at + 1) * count // 7) for at in range(7)]
-
-        def take(name, r, s):
-            if name == "own":
-                take_own()
-                chunks_from(1, count, lambda ch: hop(rep, ch, True).start())
-            else:
-                grad_got(r, s).wait_recv()
-                share(r, s)
-
-        def after(at):
-            def act(ch):
-                crossed(edge, ch).wait_recv()
-                hop_other(ch).start()
-            chunks_from(*share_of[at], act)
-
-        spread(
-            [("own", rep, other), ("near", near, fsdp), ("near", near, other),
-             ("far", far, fsdp), ("far", far, other),
-             ("last", far_edge, fsdp), ("last", far_edge, other)],
-            take, after,
-        )
-
-    @on_middle
-    def _():
-        def take(name, r, s):
-            if name == "own":
-                take_own()
-                return
-            grad_got(r, s).wait_recv()
-            grad_hop(r, s, False, name == "edge").start()
-            share(r, s)
-
-        spread(
-            [("own", rep, other), ("edge", edge, fsdp), ("far", far, fsdp),
-             ("edge", edge, other), ("far", far, other),
-             ("last", far_edge, fsdp), ("last", far_edge, other)],
-            take, lambda at: None,
-        )
 
     def clear():
         sums[fsdp * n_tp + tp] = jnp.zeros(sums.shape[1:], sums.dtype)
@@ -300,67 +248,137 @@
     def sweep(events, arrived, squared):
         places = [at * tiles // len(events) for at in range(len(events))]
 
-        def step(index, lagging):
-            def at_tile(m):
-                for place, event in zip(places, events):
-                    pl.when(m == place)(lambda: event(chunk(index)))
-                if lagging is not None:
+        def step(index):
+            ch, lagging = chunk(index), chunk(index - LAG)
+            with jax.named_scope("arrived"):
+                arrived(lagging)
+
+            @pl.loop(0, tiles)
+            def _(m):
+                for at, (place, event) in enumerate(zip(places, events)):
+                    def run():
+                        with jax.named_scope(f"event{at}"):
+                            event(ch)
+                    pl.when(m == place)(run)
+                with jax.named_scope("multiply"):
                     multiply_tile(lagging, m, squared)
-            if lagging is not None:
-                arrived(lagging)
-                pl.loop(0, tiles)(at_tile)
-            else:
-                for event in events:
-                    event(chunk(index))
-
-        start = min(count, first + LAG)
-        for index in range(start):
-            step(index, chunk(index - LAG) if index >= LAG else None)
-
-        @pl.loop(start, count)
+
+        for index in range(LAG, LAG + first):
+            step(index)
+        pl.loop(LAG + first, count)(step)
+
+        @pl.loop(count - LAG, count)
         def _(index):
-            step(index, chunk(index - LAG))
-
-        def finish(ch):
-            arrived(ch)
-            pl.loop(0, tiles)(lambda m: multiply_tile(ch, m, squared))
-        chunks_from(max(count - LAG, 0), count, finish)
+            with jax.named_scope("arrived_last"):
+                arrived(chunk(index))
+            with jax.named_scope("multiply_last"):
+                pl.loop(0, tiles)(lambda m: multiply_tile(chunk(index), m, squared))
 
     @on_edge
     def _():
+        places = {"near": near, "far": far, "last": far_edge}
+        sides = {"own": fsdp, "other": other}
+
+        def take(name, s):
+            grad_got(places[name], sides[s]).wait_recv()
+            share(places[name], sides[s])
+
+        def land(name, s, whole):
+            r = rep if name == "rep" else places[name]
+            pass_on(r, sides[s])
+            settle_later.append((r, sides[s]))
+            if whole:
+                for pair in settle_later:
+                    settle(*pair)
+                settle_later.clear()
+                turn(r)
+
+        settle_later = []
+
+        def relay(*indices):
+            for index in indices:
+                if index + early < count:
+                    hop(rep, chunk(index + early), True).start()
+                if index < count:
+                    crossed(edge, chunk(index)).wait_recv()
+                    hop_other(chunk(index)).start()
+
         def pull(r):
             def event(ch):
                 hop_got(r, ch).wait_recv()
                 cross(r, ch).start()
             return event
 
+        events = [pull(near), pull(far), pull(far_edge)]
+
+        def early_events(*indices):
+            for index in indices:
+                for event in events:
+                    event(chunk(index))
+
+        def batch(k):
+            return range(k * count // 8, (k + 1) * count // 8)
+
+        perform(
+            [
+                ("own",), ("take", "near", "own"), ("relay", *batch(0)),
+                ("take", "near", "other"), ("land", "rep", "other", True), ("relay", *batch(1)),
+                ("take", "far", "own"), ("land", "near", "own", False), ("relay", *batch(2)),
+                ("take", "far", "other"), ("land", "near", "other", True), ("relay", *batch(3)),
+                ("take", "last", "own"), ("land", "far", "own", False), ("relay", *batch(4)),
+                ("take", "last", "other"), ("land", "far", "other", True), ("relay", *batch(5)),
+                ("early", 0, 1), ("land", "last", "own", False), ("relay", *batch(6)),
+                ("early", 2), ("land", "last", "other", True), ("relay", *batch(7)),
+                ("early", 3),
+            ],
+            {"own": take_own, "take": take, "land": land, "relay": relay, "early": early_events},
+        )
+
         def arrived(ch):
             for r in (near, far, far_edge):
                 crossed(r, ch).wait_recv()
 
-        sweep([pull(near), pull(far), pull(far_edge)], arrived, False)
+        sweep(events, arrived, False)
 
     @on_middle
     def _():
-        def inward(ch):
-            hop(rep, ch, True).start()
-            hop_got(edge, ch).wait_recv()
-            hop(edge, ch, True).start()
-
-        hop_got(edge, chunk(0)).wait_recv()
-        hop(edge, chunk(0), True).start()
-        chunks_from(1, min(1 + AHEAD, count), inward)
+        places = {"edge": edge, "far": far, "last": far_edge}
+        sides = {"own": fsdp, "other": other}
+
+        def take(name, s):
+            r, s = places[name], sides[s]
+            grad_got(r, s).wait_recv()
+            grad_hop(r, s, False, name == "edge").start()
+            share(r, s)
+
+        settle_later = {}
+
+        def land(name, s):
+            r = rep if name == "rep" else places[name]
+            pass_on(r, sides[s])
+            settle_later.setdefault(name, []).append((r, sides[s]))
+            if len(settle_later[name]) == (1 if name == "rep" else 2):
+                for pair in settle_later[name]:
+                    settle(*pair)
+                turn(r)
+
+        def inward(*indices):
+            for index in indices:
+                ch = chunk(index)
+                if index >= early:
+                    hop(rep, ch, True).start()
+                hop_got(edge, ch).wait_recv()
+                hop(edge, ch, True).start()
 
         def outer(ch):
-            index = ch.index
-            if isinstance(index, int):
-                if index:
-                    hop(rep, ch, False).start()
-                    if index + AHEAD < count:
-                        inward(chunk(index + AHEAD))
-            else:
-                hop(rep, ch, False).start()
-                pl.when(index + AHEAD < count)(lambda: inward(chunk(index + AHEAD)))
+            hop(rep, ch, False).start()
+
+            @pl.when(ch.index + AHEAD < count)
+            def _():
+                ahead = chunk(ch.index + AHEAD)
+                hop(rep, ahead, True).start()
+                hop_got(edge, ahead).wait_recv()
+                hop(edge, ahead, True).start()
 
         def pull(r):
             def event(ch):
@@ -369,13 +387,35 @@
                 cross(r, ch).start()
             return event
 
+        pulls = [pull(far), pull(far_edge)]
+
+        def early_events(*indices):
+            for index in indices:
+                if index >= early:
+                    hop(rep, chunk(index), False).start()
+                for event in pulls:
+                    event(chunk(index))
+
+        perform(
+            [
+                ("own",), ("take", "far", "own"), ("take", "edge", "own"),
+                ("take", "edge", "other"), ("inward", *range(early)), ("take", "far", "other"),
+                ("land", "rep", "other"), ("take", "last", "own"), ("land", "far", "own"),
+                ("inward", *range(early, LAG)), ("take", "last", "other"), ("land", "edge", "own"),
+                ("early", 0, 1), ("inward", *range(LAG, LAG + 2)), ("land", "edge", "other"),
+                ("land", "far", "other"), ("early", 2), ("inward", LAG + 2), ("land", "last", "own"),
+                ("early", 3), ("inward", LAG + 3), ("land", "last", "other"),
+            ],
+            {"own": take_own, "take": take, "land": land, "inward": inward, "early": early_events},
+        )
+
         def arrived(ch):
             hop_other(ch).wait_recv()
             for r in (rep, far, far_edge):
                 crossed(r, ch).wait_recv()
 
         clear()
-        sweep([outer, pull(far), pull(far_edge)], arrived, True)
+        sweep([outer, *pulls], arrived, True)
 
         mine = fsdp * n_tp + tp
         peers = [(a, k) for a in range(2) for k in range(n_tp) if a or k]
@@ -389,8 +429,9 @@
 
         for at in range(len(peers)):
             exchange(at, True).start()
-        for at in range(len(peers)):
-            exchange(at, False).wait_recv()
+        with jax.named_scope("exchange"):
+            for at in range(len(peers)):
+                exchange(at, False).wait_recv()
         square_total = jnp.sum(jnp.sum(sums[...], axis=0), keepdims=True)
         factor = 1.0 / jnp.sqrt(square_total / entry_count + 1e-06)
         total_out[...] = jnp.broadcast_to(factor, total_out.shape)
@@ -401,10 +442,12 @@
         return remote(total_out, total_out, fa_send, fa_recv, {"rep": jnp.where(is_edge, near, edge)})
 
     on_middle(lambda: tell().start())
-    on_edge(lambda: tell().wait_recv())
+    with jax.named_scope("told"):
+        on_edge(lambda: tell().wait_recv())
     factor_ref[...] = total_out[...]
 
-    grad_across().wait_send()
+    with jax.named_scope("sent"):
+        grad_across().wait_send()
 
     def sent_shares(r, s):
         over_y(r, s, tp).wait_send()
@@ -542,7 +585,7 @@
     tokens, half = rows * n_rep * n_fsdp, features // n_fsdp
     held_bytes = 2 * (tokens * columns + 2 * tokens * half + half * columns + 2 * rows * columns)
     aligned = rows % 128 == 0 and columns % LANES == 0 and half % (LANES * n_tp) == 0
-    shaped = (n_rep, n_fsdp, n_tp) == (4, 2, 4) and columns >= 4 * WIDTH
+    shaped = (n_rep, n_fsdp, n_tp) == (4, 2, 4) and columns >= 12 * WIDTH
     return shaped and aligned and half % TILE == 0 and held_bytes < VMEM_LIMIT * 3 // 4
 
 

time: 116 us -> 103 us (0.89)
  Pallas kernels: 115 us -> 102 us
    pallas_call x1, Pallas kernels: 110 us -> 96.9 us  [by_kernel(): pl.pallas_call(functools.partial(gather_multiply, entry_count), out_shape...]
where the time goes in v1:
time: 103 us; the launch traced here: 102 us
  Pallas kernels  102 us (99%)
    pallas_call x1, Pallas kernels, by_kernel(): pl.pallas_call(functools.partial(gather_multiply, entry_count), out_shape...  96.9 us
    pallas_call x1, Pallas kernels, scale(): pl.pallas_call(body, out_shape=jax.ShapeDtypeStruct((half, columns), jnp....  5.58 us

profile of v1, /device:TPU:0, one launch (start us, length us, event | category | flops | bytes accessed | tf_op | source)
XLA Modules:
  0.0 102.5 jit_solution(367524596755502328)
XLA Ops:
  0.0 96.9 %shard_map.37 = (bf16[2048,3712]{1,0:T(8,128)(2,1)S(1)}, f32[8,128]{1,0:T(8,128)S(1)}) custom-call(bf16[128,3712]{1,0:T(8,128)(2,1)} %gate_ref.1, bf16[128,3712]{1,0:T(8,128)(2,1)} %up_ref.1, bf16[128,4096]{1,0:T(8,128)(2,1)} %grad_ref.1), custom_call_target="tpu_custom_call" | custom-call | tf_op jit(solution)/shard_map/pallas_call | solution.py:503
  96.9 5.6 %shard_map.38 = bf16[2048,3712]{1,0:T(8,128)(2,1)} custom-call(bf16[2048,3712]{1,0:T(8,128)(2,1)S(1)} %get-tuple-element.7.summed_ref, f32[8,128]{1,0:T(8,128)S(1)} %get-tuple-element.8.factor_ref), custom_call_target="tpu_custom_call" | custom-call | tf_op jit(solution)/shard_map/pallas_call | solution.py:561

commit v2 on v1

--- a/solution.py
+++ b/solution.py
@@ -14,6 +14,8 @@
 TILE = 1024
 LAG = 4
 AHEAD = 4
+FILL = 3
+EXTRA = (6, 10)
 
 
 class Chunk:
@@ -27,24 +29,22 @@
 
 
 def chunking(columns):
-    head = columns % WIDTH
-    first = 1 if head else 0
-    count = first + columns // WIDTH
+    full, rest = columns // WIDTH, columns % WIDTH
 
     def chunk(index):
-        if isinstance(index, int) and index < first:
-            return Chunk(index, 0, head)
-        return Chunk(index, head + (index - first) * WIDTH, WIDTH)
-
-    return first, count, chunk
+        if isinstance(index, int) and index == full:
+            return Chunk(index, full * WIDTH, rest)
+        return Chunk(index, index * WIDTH, WIDTH)
+
+    return full, full + (1 if rest else 0), chunk
 
 
 def gather_multiply(
     entry_count, gate_ref, up_ref, grad_ref, out_ref, factor_ref,
-    held, grads, turned, gate_in, up_in, sums, total_out,
+    held, grads, turned, gate_in, up_in, across_in, sums, total_out,
     local_sem, gx_send, gx_recv, gz_recv, gz_out, gz_in, gy_send, gy_recv,
     gs_send, gs_recv, gf_send, gf_recv,
-    z_recv, z_out, z_in, zo_recv, zo_send, x_send, x_recv,
+    z_recv, z_out, z_in, zo_recv, zo_send, ze_recv, ze_send, x_send, x_recv,
     sq_send, sq_recv, fa_send, fa_recv,
 ):
     rep = lax.axis_index("rep")
@@ -54,7 +54,7 @@
     half = grads.shape[1]
     n_tp = 4
     quarter = half // n_tp
-    first, count, chunk = chunking(columns)
+    full, count, chunk = chunking(columns)
     other = 1 - fsdp
     side = rep // 2
     edge, near, far, far_edge = 3 * side, 1 + side, 2 - side, 3 - 3 * side
@@ -83,20 +83,17 @@
             grad_ref.at[:, pl.ds(pl.multiple_of(fsdp * half, LANES), half)],
             grads.at[rows_of(rep, fsdp), :], local_sem.at[2],
         ),
+        pltpu.make_async_copy(
+            grad_ref.at[:, pl.ds(pl.multiple_of(other * half + tp * quarter, LANES), quarter)],
+            across_in, local_sem.at[3],
+        ),
     ]
     for load in loads:
         load.start()
 
     barrier = pltpu.get_barrier_semaphore()
-    for k in range(n_tp):
-        if k:
-            pl.semaphore_signal(
-                barrier, inc=1, device_id={"tp": lax.rem(tp + k, n_tp)}, device_id_type=MESH
-            )
-        pl.semaphore_signal(
-            barrier, inc=1, device_id={"fsdp": other, "tp": lax.rem(tp + k, n_tp)},
-            device_id_type=MESH,
-        )
+    for peer in ({"fsdp": other}, {"tp": sibling}, {"tp": opposite}):
+        pl.semaphore_signal(barrier, inc=1, device_id=peer, device_id_type=MESH)
     pl.semaphore_signal(barrier, inc=1, device_id={"rep": inner}, device_id_type=MESH)
 
     @pl.when(jnp.logical_not(is_edge))
@@ -104,8 +101,8 @@
         pl.semaphore_signal(barrier, inc=1, device_id={"rep": edge}, device_id_type=MESH)
 
     with jax.named_scope("load"):
-        loads[0].wait()
-        loads[1].wait()
+        for load in loads:
+            load.wait()
 
     @pl.loop(0, columns // LANES)
     def _(at):
@@ -116,22 +113,18 @@
         ).astype(held.dtype)
 
     with jax.named_scope("barrier"):
-        pl.semaphore_wait(barrier, 2 * n_tp + jnp.where(is_edge, 0, 1))
+        pl.semaphore_wait(barrier, 4 + jnp.where(is_edge, 0, 1))
 
     def grad_across():
-        src = grad_ref.at[:, pl.ds(pl.multiple_of(other * half + tp * quarter, LANES), quarter)]
-        return remote(src, grads.at[rows_of(rep, fsdp), quarter_of(tp)], gx_send, gx_recv, {"fsdp": other})
+        return remote(across_in, grads.at[rows_of(rep, fsdp), quarter_of(tp)], gx_send, gx_recv, {"fsdp": other})
 
     def grad_spot(r, s, t):
         return grads.at[rows_of(r, s), quarter_of(t)]
 
-    def grad_hop(r, s, own, inward):
+    def grad_hop(r, s, inward):
         spot = grad_spot(r, s, tp)
-        src = spot
-        if own:
-            src = grad_ref.at[:, pl.ds(pl.multiple_of(fsdp * half + tp * quarter, LANES), quarter)]
         to = inner if inward else edge
-        return remote(src, spot, (gz_in if inward else gz_out).at[r, s], gz_recv.at[r, s], {"rep": to})
+        return remote(spot, spot, (gz_in if inward else gz_out).at[r, s], gz_recv.at[r, s], {"rep": to})
 
     def grad_got(r, s):
         spot = grad_spot(r, s, tp)
@@ -152,23 +145,45 @@
     def hop(r, ch, inward):
         spot = held.at[rows_of(r, fsdp), ch.cols]
         to = inner if inward else edge
-        return remote(spot, spot, (z_in if inward else z_out).at[r, ch.index], z_recv.at[r, ch.index], {"rep": to})
+        return remote(spot, spot, (z_in if inward else z_out).at[r], z_recv.at[r, ch.index], {"rep": to})
 
     def hop_got(r, ch):
         spot = held.at[rows_of(r, fsdp), ch.cols]
-        return remote(spot, spot, z_in.at[r, ch.index], z_recv.at[r, ch.index], {"rep": inner})
+        return remote(spot, spot, z_in.at[r], z_recv.at[r, ch.index], {"rep": inner})
 
     def hop_other(ch):
         spot = held.at[rows_of(edge, other), ch.cols]
-        return remote(spot, spot, zo_send.at[ch.index], zo_recv.at[ch.index], {"rep": inner})
+        return remote(spot, spot, zo_send, zo_recv.at[ch.index], {"rep": inner})
 
     def cross(r, ch):
         spot = held.at[rows_of(r, fsdp), ch.cols]
-        return remote(spot, spot, x_send.at[r, ch.index], x_recv.at[r, ch.index], {"fsdp": other})
+        return remote(spot, spot, x_send.at[r], x_recv.at[r, ch.index], {"fsdp": other})
 
     def crossed(r, ch):
         spot = held.at[rows_of(r, other), ch.cols]
-        return remote(spot, spot, x_send.at[r, ch.index], x_recv.at[r, ch.index], {"fsdp": other})
+        return remote(spot, spot, x_send.at[r], x_recv.at[r, ch.index], {"fsdp": other})
+
+    def hop_extra(ch):
+        spot = held.at[rows_of(near, other), ch.cols]
+        return remote(spot, spot, ze_send, ze_recv.at[ch.index], {"rep": jnp.where(is_edge, near, edge)})
+
+    def all_sent(r, s, width, send):
+        spot = held.at[rows_of(r, s), pl.ds(0, width)]
+        remote(spot, spot, send, gx_recv, {"fsdp": other}).wait_send()
+
+    def when_extra(ch, act, otherwise=None):
+        if isinstance(ch.index, int):
+            if ch.index in EXTRA:
+                act()
+            elif otherwise is not None:
+                otherwise()
+            return
+        hit = ch.index == EXTRA[0]
+        for index in EXTRA[1:]:
+            hit = jnp.logical_or(hit, ch.index == index)
+        pl.when(hit)(act)
+        if otherwise is not None:
+            pl.when(jnp.logical_not(hit))(otherwise)
 
     def on_edge(act):
         pl.when(is_edge)(act)
@@ -177,20 +192,19 @@
         pl.when(jnp.logical_not(is_edge))(act)
 
     def chunks_from(low, high, act):
-        while low < high and low < first:
-            act(chunk(low))
-            low += 1
-        if low < high:
-            @pl.loop(low, high)
+        if low < min(high, full):
+            @pl.loop(low, min(high, full))
             def _(index):
                 act(chunk(index))
+        if full < count == high:
+            act(chunk(full))
 
     grad_across().start()
-    grad_hop(rep, fsdp, True, True).start()
-    on_middle(lambda: grad_hop(rep, fsdp, True, False).start())
+    grad_hop(rep, fsdp, True).start()
+    on_middle(lambda: grad_hop(rep, fsdp, False).start())
 
     chunks_from(0, count, lambda ch: cross(rep, ch).start())
-    early = first + 1
+    early = 2
     chunks_from(0, early, lambda ch: hop(rep, ch, True).start())
     on_middle(lambda: chunks_from(0, early, lambda ch: hop(rep, ch, False).start()))
 
@@ -218,8 +232,8 @@
 
     def take_own():
         grad_across().wait_recv()
-        grad_hop(rep, other, False, True).start()
-        on_middle(lambda: grad_hop(rep, other, False, False).start())
+        grad_hop(rep, other, True).start()
+        on_middle(lambda: grad_hop(rep, other, False).start())
         share(rep, other)
 
     def perform(plan, acts):
@@ -227,7 +241,18 @@
             with jax.named_scope(f"{name}{at}"):
                 acts[name](*args)
 
-    loads[2].wait()
+    def sent_shares(r, s):
+        over_y(r, s, tp).wait_send()
+        to_sibling(r, s, tp).wait_send()
+        pass_sibling(r, s, opposite).wait_send()
+
+    def sent_first():
+        grad_across().wait_send()
+        sent_shares(rep, other)
+        grad_hop(rep, fsdp, True).wait_send()
+        grad_hop(rep, other, True).wait_send()
+        all_sent(rep, fsdp, columns, x_send.at[rep])
+        all_sent(rep, fsdp, columns, z_in.at[rep])
 
     def clear():
         sums[fsdp * n_tp + tp] = jnp.zeros(sums.shape[1:], sums.dtype)
@@ -245,7 +270,7 @@
 
     tiles = half // TILE
 
-    def sweep(events, arrived, squared):
+    def sweep(events, arrived, between, squared):
         places = [at * tiles // len(events) for at in range(len(events))]
 
         def step(index):
@@ -263,16 +288,17 @@
                 with jax.named_scope("multiply"):
                     multiply_tile(lagging, m, squared)
 
-        for index in range(LAG, LAG + first):
+        pl.loop(LAG, full - 1)(step)
+        between()
+        for index in range(full - 1, count):
             step(index)
-        pl.loop(LAG + first, count)(step)
-
-        @pl.loop(count - LAG, count)
-        def _(index):
+
+        def finish(ch):
             with jax.named_scope("arrived_last"):
-                arrived(chunk(index))
+                arrived(ch)
             with jax.named_scope("multiply_last"):
-                pl.loop(0, tiles)(lambda m: multiply_tile(chunk(index), m, squared))
+                pl.loop(0, tiles)(lambda m: multiply_tile(ch, m, squared))
+        chunks_from(count - LAG, count, finish)
 
     @on_edge
     def _():
@@ -309,7 +335,11 @@
                 cross(r, ch).start()
             return event
 
-        events = [pull(near), pull(far), pull(far_edge)]
+        def pull_near(ch):
+            hop_got(near, ch).wait_recv()
+            when_extra(ch, lambda: None, lambda: cross(near, ch).start())
+
+        events = [pull_near, pull(far), pull(far_edge)]
 
         def early_events(*indices):
             for index in indices:
@@ -335,10 +365,23 @@
         )
 
         def arrived(ch):
+            when_extra(
+                ch, lambda: hop_extra(ch).wait_recv(), lambda: crossed(near, ch).wait_recv()
+            )
+            for r in (far, far_edge):
+                crossed(r, ch).wait_recv()
+
+        def between():
+            sent_first()
             for r in (near, far, far_edge):
-                crossed(r, ch).wait_recv()
-
-        sweep(events, arrived, False)
+                for s in (fsdp, other):
+                    sent_shares(r, s)
+            all_sent(rep, other, columns, zo_send)
+
+        sweep(events, arrived, between, False)
+        all_sent(near, fsdp, columns - len(EXTRA) * WIDTH, x_send.at[near])
+        for r in (far, far_edge):
+            all_sent(r, fsdp, columns, x_send.at[r])
 
     @on_middle
     def _():
@@ -348,7 +391,7 @@
         def take(name, s):
             r, s = places[name], sides[s]
             grad_got(r, s).wait_recv()
-            grad_hop(r, s, False, name == "edge").start()
+            grad_hop(r, s, name == "edge").start()
             share(r, s)
 
         settle_later = {}
@@ -365,20 +408,34 @@
         def inward(*indices):
             for index in indices:
                 ch = chunk(index)
-                if index >= early:
+                if not isinstance(index, int) or index >= early:
                     hop(rep, ch, True).start()
                 hop_got(edge, ch).wait_recv()
                 hop(edge, ch, True).start()
 
+        def fill(*indices):
+            for index in indices:
+                hop(rep, chunk(index), False).start()
+
         def outer(ch):
-            hop(rep, ch, False).start()
-
-            @pl.when(ch.index + AHEAD < count)
-            def _():
-                ahead = chunk(ch.index + AHEAD)
-                hop(rep, ahead, True).start()
-                hop_got(edge, ahead).wait_recv()
-                hop(edge, ahead, True).start()
+            if isinstance(ch.index, int):
+                if ch.index + FILL < count:
+                    fill(ch.index + FILL)
+            else:
+                pl.when(ch.index + FILL < full)(lambda: fill(ch.index + FILL))
+                if full < count:
+                    pl.when(ch.index + FILL == full)(lambda: fill(full))
+            when_extra(ch, lambda: (crossed(rep, ch).wait_recv(), hop_extra(ch).start()) and None)
+            follow(ch.index + AHEAD)
+
+        def follow(index):
+            if isinstance(index, int):
+                if index < count:
+                    inward(index)
+                return
+            pl.when(index < full)(lambda: inward(index))
+            if full < count:
+                pl.when(index == full)(lambda: inward(full))
 
         def pull(r):
             def event(ch):
@@ -392,30 +449,32 @@
         def early_events(*indices):
             for index in indices:
                 if index >= early:
-                    hop(rep, chunk(index), False).start()
+                    fill(index + FILL)
                 for event in pulls:
                     event(chunk(index))
 
         perform(
             [
-                ("own",), ("take", "far", "own"), ("take", "edge", "own"),
+                ("own",), ("take", "far", "own"), ("fill", early), ("take", "edge", "own"),
                 ("take", "edge", "other"), ("inward", *range(early)), ("take", "far", "other"),
-                ("land", "rep", "other"), ("take", "last", "own"), ("land", "far", "own"),
+                ("fill", early + 1), ("land", "rep", "other"), ("take", "last", "own"),
+                ("fill", early + 2), ("land", "far", "own"),
                 ("inward", *range(early, LAG)), ("take", "last", "other"), ("land", "edge", "own"),
                 ("early", 0, 1), ("inward", *range(LAG, LAG + 2)), ("land", "edge", "other"),
                 ("land", "far", "other"), ("early", 2), ("inward", LAG + 2), ("land", "last", "own"),
                 ("early", 3), ("inward", LAG + 3), ("land", "last", "other"),
             ],
-            {"own": take_own, "take": take, "land": land, "inward": inward, "early": early_events},
+            {"own": take_own, "take": take, "land": land, "inward": inward, "early": early_events, "fill": fill},
         )
 
         def arrived(ch):
             hop_other(ch).wait_recv()
-            for r in (rep, far, far_edge):
+            when_extra(ch, lambda: None, lambda: crossed(rep, ch).wait_recv())
+            for r in (far, far_edge):
                 crossed(r, ch).wait_recv()
 
         clear()
-        sweep([outer, *pulls], arrived, True)
+        sweep([outer, *pulls], arrived, lambda: None, True)
 
         mine = fsdp * n_tp + tp
         peers = [(a, k) for a in range(2) for k in range(n_tp) if a or k]
@@ -446,60 +505,34 @@
         on_edge(lambda: tell().wait_recv())
     factor_ref[...] = total_out[...]
 
-    with jax.named_scope("sent"):
-        grad_across().wait_send()
-
-    def sent_shares(r, s):
-        over_y(r, s, tp).wait_send()
-        to_sibling(r, s, tp).wait_send()
-        pass_sibling(r, s, opposite).wait_send()
-
-    sent_shares(rep, other)
-    grad_hop(rep, fsdp, True, True).wait_send()
-    grad_hop(rep, other, False, True).wait_send()
-    chunks_from(0, count, lambda ch: cross(rep, ch).wait_send())
-
-    @on_edge
-    def _():
-        for r in (near, far, far_edge):
-            for s in (fsdp, other):
-                sent_shares(r, s)
-
-        def sent(ch):
-            hop(rep, ch, True).wait_send()
-            hop_other(ch).wait_send()
-            for r in (near, far, far_edge):
-                cross(r, ch).wait_send()
-        chunks_from(0, count, sent)
-
     @on_middle
     def _():
         tell().wait_send()
-        for s, own in ((fsdp, True), (other, False)):
-            grad_hop(rep, s, own, False).wait_send()
-            grad_hop(edge, s, False, True).wait_send()
+        sent_first()
+        for s in (fsdp, other):
+            grad_hop(rep, s, False).wait_send()
+            grad_hop(edge, s, True).wait_send()
             for r in (edge, far, far_edge):
                 sent_shares(r, s)
             for r in (far, far_edge):
-                grad_hop(r, s, False, False).wait_send()
-
-        def sent(ch):
-            for r in (rep, edge):
-                hop(r, ch, True).wait_send()
-            for r in (rep, far, far_edge):
-                hop(r, ch, False).wait_send()
-            for r in (far, far_edge):
-                cross(r, ch).wait_send()
-        chunks_from(0, count, sent)
+                grad_hop(r, s, False).wait_send()
+        all_sent(edge, fsdp, columns, z_in.at[edge])
+        for r in (rep, far, far_edge):
+            all_sent(r, fsdp, columns, z_out.at[r])
+        for r in (far, far_edge):
+            all_sent(r, fsdp, columns, x_send.at[r])
+        all_sent(rep, other, len(EXTRA) * WIDTH, ze_send)
 
 
 def by_kernel(n_rep, n_tp, entry_count, gate_pre, up_pre, out_grad):
     rows, columns = gate_pre.shape
     tokens = rows * n_rep * 2
     half = out_grad.shape[1] // 2
+    quarter = half // n_tp
     count = chunking(columns)[1]
     dma = pltpu.SemaphoreType.DMA
-    block, piece = dma((n_rep, 2)), dma((n_rep, count))
+    block, piece, line = dma((n_rep, 2)), dma((n_rep, count)), dma((count,))
+    whole = dma((n_rep,))
     return pl.pallas_call(
         functools.partial(gather_multiply, entry_count),
         out_shape=(
@@ -514,11 +547,12 @@
             pltpu.VMEM((half, tokens), jnp.bfloat16),
             pltpu.VMEM((rows, columns), jnp.bfloat16),
             pltpu.VMEM((rows, columns), jnp.bfloat16),
+            pltpu.VMEM((rows, quarter), jnp.bfloat16),
             pltpu.VMEM((2 * n_tp, 8, LANES), jnp.float32),
             pltpu.VMEM((8, LANES), jnp.float32),
-            dma((3,)), dma, dma, block, block, block, block, block,
+            dma((4,)), dma, dma, block, block, block, block, block,
             block, block, block, block,
-            piece, piece, piece, dma((count,)), dma((count,)), piece, piece,
+            piece, whole, whole, line, dma, line, dma, whole, piece,
             dma((2 * n_tp - 1,)), dma((2 * n_tp - 1,)), dma, dma,
         ],
         compiler_params=pltpu.CompilerParams(

time: 103 us -> 105 us (1.019)
  Pallas kernels: 102 us -> 105 us
    pallas_call x1, Pallas kernels: 96.9 us -> 98.9 us  [by_kernel(): pl.pallas_call(functools.partial(gather_multiply, entry_count), out_shape...]
where the time goes in v2:
time: 105 us
  Pallas kernels  105 us (100%)
    pallas_call x1, Pallas kernels, by_kernel(): pl.pallas_call(functools.partial(gather_multiply, entry_count), out_shape...  98.9 us
    pallas_call x1, Pallas kernels, scale(): pl.pallas_call(body, out_shape=jax.ShapeDtypeStruct((half, columns), jnp....  5.58 us

profile of v2, /device:TPU:0, one launch (start us, length us, event | category | flops | bytes accessed | tf_op | source)
XLA Modules:
  0.0 104.5 jit_solution(4779603647589502882)
XLA Ops:
  0.0 98.9 %shard_map.37 = (bf16[2048,3712]{1,0:T(8,128)(2,1)S(1)}, f32[8,128]{1,0:T(8,128)S(1)}) custom-call(bf16[128,3712]{1,0:T(8,128)(2,1)} %gate_ref.1, bf16[128,3712]{1,0:T(8,128)(2,1)} %up_ref.1, bf16[128,4096]{1,0:T(8,128)(2,1)} %grad_ref.1), custom_call_target="tpu_custom_call" | custom-call | tf_op jit(solution)/shard_map/pallas_call | solution.py:536
  98.9 5.6 %shard_map.38 = bf16[2048,3712]{1,0:T(8,128)(2,1)} custom-call(bf16[2048,3712]{1,0:T(8,128)(2,1)S(1)} %get-tuple-element.7.summed_ref, f32[8,128]{1,0:T(8,128)S(1)} %get-tuple-element.8.factor_ref), custom_call_target="tpu_custom_call" | custom-call | tf_op jit(solution)/shard_map/pallas_call | solution.py:595

commit v3 on v2

--- a/solution.py
+++ b/solution.py
@@ -15,7 +15,7 @@
 LAG = 4
 AHEAD = 4
 FILL = 3
-EXTRA = (6, 10)
+EXTRA = (8,)
 
 
 class Chunk:
@@ -339,11 +339,27 @@
             hop_got(near, ch).wait_recv()
             when_extra(ch, lambda: None, lambda: cross(near, ch).start())
 
-        events = [pull_near, pull(far), pull(far_edge)]
+        pulls = [pull(far), pull(far_edge)]
+
+        def near_at(*indices):
+            for index in indices:
+                pull_near(chunk(index))
+
+        def near_ahead(ch):
+            index = ch.index + FILL
+            if isinstance(index, int):
+                if index < count:
+                    near_at(index)
+                return
+            pl.when(index < full)(lambda: near_at(index))
+            if full < count:
+                pl.when(index == full)(lambda: near_at(full))
 
         def early_events(*indices):
             for index in indices:
-                for event in events:
+                if index >= early:
+                    near_at(index + FILL)
+                for event in pulls:
                     event(chunk(index))
 
         def batch(k):
@@ -351,17 +367,17 @@
 
         perform(
             [
-                ("own",), ("take", "near", "own"), ("relay", *batch(0)),
+                ("own",), ("take", "near", "own"), ("relay", *batch(0)), ("near", *range(early)),
                 ("take", "near", "other"), ("land", "rep", "other", True), ("relay", *batch(1)),
-                ("take", "far", "own"), ("land", "near", "own", False), ("relay", *batch(2)),
-                ("take", "far", "other"), ("land", "near", "other", True), ("relay", *batch(3)),
-                ("take", "last", "own"), ("land", "far", "own", False), ("relay", *batch(4)),
+                ("take", "far", "own"), ("near", early), ("land", "near", "own", False),
+                ("relay", *batch(2)), ("take", "far", "other"), ("near", early + 1),
+                ("land", "near", "other", True), ("relay", *batch(3)), ("take", "last", "own"),
+                ("near", early + 2), ("land", "far", "own", False), ("relay", *batch(4)),
                 ("take", "last", "other"), ("land", "far", "other", True), ("relay", *batch(5)),
-                ("early", 0, 1), ("land", "last", "own", False), ("relay", *batch(6)),
-                ("early", 2), ("land", "last", "other", True), ("relay", *batch(7)),
-                ("early", 3),
+                ("early", 0), ("relay", *batch(6)), ("early", 1), ("land", "last", "own", False),
+                ("relay", *batch(7)), ("early", 2), ("land", "last", "other", True), ("early", 3),
             ],
-            {"own": take_own, "take": take, "land": land, "relay": relay, "early": early_events},
+            {"own": take_own, "take": take, "land": land, "relay": relay, "early": early_events, "near": near_at},
         )
 
         def arrived(ch):
@@ -378,7 +394,7 @@
                     sent_shares(r, s)
             all_sent(rep, other, columns, zo_send)
 
-        sweep(events, arrived, between, False)
+        sweep([near_ahead, *pulls], arrived, between, False)
         all_sent(near, fsdp, columns - len(EXTRA) * WIDTH, x_send.at[near])
         for r in (far, far_edge):
             all_sent(r, fsdp, columns, x_send.at[r])

time: 105 us -> 101 us (0.962)
  Pallas kernels: 105 us -> 101 us
    pallas_call x1, Pallas kernels: 98.9 us -> 95 us  [by_kernel(): pl.pallas_call(functools.partial(gather_multiply, entry_count), out_shape...]
where the time goes in v3:
time: 101 us
  Pallas kernels  101 us (100%)
    pallas_call x1, Pallas kernels, by_kernel(): pl.pallas_call(functools.partial(gather_multiply, entry_count), out_shape...  95 us
    pallas_call x1, Pallas kernels, scale(): pl.pallas_call(body, out_shape=jax.ShapeDtypeStruct((half, columns), jnp....  5.58 us

profile of v3, /device:TPU:0, one launch (start us, length us, event | category | flops | bytes accessed | tf_op | source)
XLA Modules:
  0.0 100.6 jit_solution(11636541082377807784)
XLA Ops:
  0.0 95.0 %shard_map.37 = (bf16[2048,3712]{1,0:T(8,128)(2,1)S(1)}, f32[8,128]{1,0:T(8,128)S(1)}) custom-call(bf16[128,3712]{1,0:T(8,128)(2,1)} %gate_ref.1, bf16[128,3712]{1,0:T(8,128)(2,1)} %up_ref.1, bf16[128,4096]{1,0:T(8,128)(2,1)} %grad_ref.1), custom_call_target="tpu_custom_call" | custom-call | tf_op jit(solution)/shard_map/pallas_call | solution.py:552
  95.0 5.6 %shard_map.38 = bf16[2048,3712]{1,0:T(8,128)(2,1)} custom-call(bf16[2048,3712]{1,0:T(8,128)(2,1)S(1)} %get-tuple-element.7.summed_ref, f32[8,128]{1,0:T(8,128)S(1)} %get-tuple-element.8.factor_ref), custom_call_target="tpu_custom_call" | custom-call | tf_op jit(solution)/shard_map/pallas_call | solution.py:611

commit v4 on v3

--- a/solution.py
+++ b/solution.py
@@ -13,9 +13,10 @@
 WIDTH = 256
 TILE = 1024
 LAG = 4
+EDGE_LAG = 2
 AHEAD = 4
 FILL = 3
-EXTRA = (8,)
+EXTRAS = 2
 
 
 class Chunk:
@@ -55,6 +56,8 @@
     n_tp = 4
     quarter = half // n_tp
     full, count, chunk = chunking(columns)
+    extras = range(count - EXTRAS, count)
+    extra_columns = columns - extras[0] * WIDTH
     other = 1 - fsdp
     side = rep // 2
     edge, near, far, far_edge = 3 * side, 1 + side, 2 - side, 3 - 3 * side
@@ -171,19 +174,12 @@
         spot = held.at[rows_of(r, s), pl.ds(0, width)]
         remote(spot, spot, send, gx_recv, {"fsdp": other}).wait_send()
 
-    def when_extra(ch, act, otherwise=None):
+    def when_extra(ch, act, otherwise):
         if isinstance(ch.index, int):
-            if ch.index in EXTRA:
-                act()
-            elif otherwise is not None:
-                otherwise()
+            act() if ch.index in extras else otherwise()
             return
-        hit = ch.index == EXTRA[0]
-        for index in EXTRA[1:]:
-            hit = jnp.logical_or(hit, ch.index == index)
-        pl.when(hit)(act)
-        if otherwise is not None:
-            pl.when(jnp.logical_not(hit))(otherwise)
+        pl.when(ch.index >= extras[0])(act)
+        pl.when(ch.index < extras[0])(otherwise)
 
     def on_edge(act):
         pl.when(is_edge)(act)
@@ -270,11 +266,17 @@
 
     tiles = half // TILE
 
-    def sweep(events, arrived, between, squared):
+    def finish(ch, arrived, squared):
+        with jax.named_scope("arrived_last"):
+            arrived(ch)
+        with jax.named_scope("multiply_last"):
+            pl.loop(0, tiles)(lambda m: multiply_tile(ch, m, squared))
+
+    def sweep(events, arrived, between, ended, lag, squared):
         places = [at * tiles // len(events) for at in range(len(events))]
 
         def step(index):
-            ch, lagging = chunk(index), chunk(index - LAG)
+            ch, lagging = chunk(index), chunk(index - lag)
             with jax.named_scope("arrived"):
                 arrived(lagging)
 
@@ -292,13 +294,8 @@
         between()
         for index in range(full - 1, count):
             step(index)
-
-        def finish(ch):
-            with jax.named_scope("arrived_last"):
-                arrived(ch)
-            with jax.named_scope("multiply_last"):
-                pl.loop(0, tiles)(lambda m: multiply_tile(ch, m, squared))
-        chunks_from(count - LAG, count, finish)
+        ended()
+        chunks_from(count - lag, count, lambda ch: finish(ch, arrived, squared))
 
     @on_edge
     def _():
@@ -361,6 +358,16 @@
                     near_at(index + FILL)
                 for event in pulls:
                     event(chunk(index))
+
+        def arrived(ch):
+            when_extra(
+                ch, lambda: hop_extra(ch).wait_recv(), lambda: crossed(near, ch).wait_recv()
+            )
+            for r in (far, far_edge):
+                crossed(r, ch).wait_recv()
+
+        def compute(index):
+            finish(chunk(index), arrived, False)
 
         def batch(k):
             return range(k * count // 8, (k + 1) * count // 8)
@@ -375,17 +382,12 @@
                 ("near", early + 2), ("land", "far", "own", False), ("relay", *batch(4)),
                 ("take", "last", "other"), ("land", "far", "other", True), ("relay", *batch(5)),
                 ("early", 0), ("relay", *batch(6)), ("early", 1), ("land", "last", "own", False),
-                ("relay", *batch(7)), ("early", 2), ("land", "last", "other", True), ("early", 3),
+                ("relay", *batch(7)), ("early", 2), ("land", "last", "other", True),
+                ("compute", 0), ("early", 3), ("compute", 1),
             ],
-            {"own": take_own, "take": take, "land": land, "relay": relay, "early": early_events, "near": near_at},
+            {"own": take_own, "take": take, "land": land, "relay": relay, "early": early_events, "near": near_at,
+             "compute": compute},
         )
-
-        def arrived(ch):
-            when_extra(
-                ch, lambda: hop_extra(ch).wait_recv(), lambda: crossed(near, ch).wait_recv()
-            )
-            for r in (far, far_edge):
-                crossed(r, ch).wait_recv()
 
         def between():
             sent_first()
@@ -394,8 +396,8 @@
                     sent_shares(r, s)
             all_sent(rep, other, columns, zo_send)
 
-        sweep([near_ahead, *pulls], arrived, between, False)
-        all_sent(near, fsdp, columns - len(EXTRA) * WIDTH, x_send.at[near])
+        sweep([near_ahead, *pulls], arrived, between, lambda: None, EDGE_LAG, False)
+        all_sent(near, fsdp, columns - extra_columns, x_send.at[near])
         for r in (far, far_edge):
             all_sent(r, fsdp, columns, x_send.at[r])
 
@@ -441,7 +443,6 @@
                 pl.when(ch.index + FILL < full)(lambda: fill(ch.index + FILL))
                 if full < count:
                     pl.when(ch.index + FILL == full)(lambda: fill(full))
-            when_extra(ch, lambda: (crossed(rep, ch).wait_recv(), hop_extra(ch).start()) and None)
             follow(ch.index + AHEAD)
 
         def follow(index):
@@ -490,7 +491,13 @@
                 crossed(r, ch).wait_recv()
 
         clear()
-        sweep([outer, *pulls], arrived, lambda: None, True)
+
+        def ended():
+            for index in extras:
+                crossed(rep, chunk(index)).wait_recv()
+                hop_extra(chunk(index)).start()
+
+        sweep([outer, *pulls], arrived, lambda: None, ended, LAG, True)
 
         mine = fsdp * n_tp + tp
         peers = [(a, k) for a in range(2) for k in range(n_tp) if a or k]
@@ -537,7 +544,7 @@
             all_sent(r, fsdp, columns, z_out.at[r])
         for r in (far, far_edge):
             all_sent(r, fsdp, columns, x_send.at[r])
-        all_sent(rep, other, len(EXTRA) * WIDTH, ze_send)
+        all_sent(rep, other, extra_columns, ze_send)
 
 
 def by_kernel(n_rep, n_tp, entry_count, gate_pre, up_pre, out_grad):

time: 101 us -> 98.3 us (0.973)
  Pallas kernels: 101 us -> 98.2 us
    pallas_call x1, Pallas kernels: 95 us -> 92.6 us  [by_kernel(): pl.pallas_call(functools.partial(gather_multiply, entry_count), out_shape...]
where the time goes in v4:
time: 98.3 us; the launch traced here: 98.2 us
  Pallas kernels  98.2 us (100%)
    pallas_call x1, Pallas kernels, by_kernel(): pl.pallas_call(functools.partial(gather_multiply, entry_count), out_shape...  92.6 us
    pallas_call x1, Pallas kernels, scale(): pl.pallas_call(body, out_shape=jax.ShapeDtypeStruct((half, columns), jnp....  5.58 us

profile of v4, /device:TPU:0, one launch (start us, length us, event | category | flops | bytes accessed | tf_op | source)
XLA Modules:
  0.0 98.2 jit_solution(926403591468656016)
XLA Ops:
  0.0 92.6 %shard_map.37 = (bf16[2048,3712]{1,0:T(8,128)(2,1)S(1)}, f32[8,128]{1,0:T(8,128)S(1)}) custom-call(bf16[128,3712]{1,0:T(8,128)(2,1)} %gate_ref.1, bf16[128,3712]{1,0:T(8,128)(2,1)} %up_ref.1, bf16[128,4096]{1,0:T(8,128)(2,1)} %grad_ref.1), custom_call_target="tpu_custom_call" | custom-call | tf_op jit(solution)/shard_map/pallas_call | solution.py:559
  92.6 5.6 %shard_map.38 = bf16[2048,3712]{1,0:T(8,128)(2,1)} custom-call(bf16[2048,3712]{1,0:T(8,128)(2,1)S(1)} %get-tuple-element.7.summed_ref, f32[8,128]{1,0:T(8,128)S(1)} %get-tuple-element.8.factor_ref), custom_call_target="tpu_custom_call" | custom-call | tf_op jit(solution)/shard_map/pallas_call | solution.py:618

commit v5 on v4

--- a/solution.py
+++ b/solution.py
@@ -16,7 +16,7 @@
 EDGE_LAG = 2
 AHEAD = 4
 FILL = 3
-EXTRAS = 2
+EXTRA = 8
 
 
 class Chunk:
@@ -43,9 +43,10 @@
 def gather_multiply(
     entry_count, gate_ref, up_ref, grad_ref, out_ref, factor_ref,
     held, grads, turned, gate_in, up_in, across_in, sums, total_out,
+    middle_part, end_part,
     local_sem, gx_send, gx_recv, gz_recv, gz_out, gz_in, gy_send, gy_recv,
     gs_send, gs_recv, gf_send, gf_recv,
-    z_recv, z_out, z_in, zo_recv, zo_send, ze_recv, ze_send, x_send, x_recv,
+    z_recv, z_out, z_in, zo_send, ze_send, x_send, xn_send, x_recv,
     sq_send, sq_recv, fa_send, fa_recv,
 ):
     rep = lax.axis_index("rep")
@@ -56,8 +57,8 @@
     n_tp = 4
     quarter = half // n_tp
     full, count, chunk = chunking(columns)
-    extras = range(count - EXTRAS, count)
-    extra_columns = columns - extras[0] * WIDTH
+    extras = (EXTRA, count - 1)
+    extra_columns = WIDTH + chunk(count - 1).size
     other = 1 - fsdp
     side = rep // 2
     edge, near, far, far_edge = 3 * side, 1 + side, 2 - side, 3 - 3 * side
@@ -127,59 +128,59 @@
     def grad_hop(r, s, inward):
         spot = grad_spot(r, s, tp)
         to = inner if inward else edge
-        return remote(spot, spot, (gz_in if inward else gz_out).at[r, s], gz_recv.at[r, s], {"rep": to})
+        return remote(spot, spot, (gz_in if inward else gz_out), gz_recv.at[r, s], {"rep": to})
 
     def grad_got(r, s):
         spot = grad_spot(r, s, tp)
-        return remote(spot, spot, gz_in.at[r, s], gz_recv.at[r, s], {"rep": inner})
+        return remote(spot, spot, gz_in, gz_recv.at[r, s], {"rep": inner})
 
     def over_y(r, s, t):
         spot = grad_spot(r, s, t)
-        return remote(spot, spot, gy_send.at[r, s], gy_recv.at[r, s], {"tp": opposite})
+        return remote(spot, spot, gy_send, gy_recv.at[r, s], {"tp": opposite})
 
     def to_sibling(r, s, t):
         spot = grad_spot(r, s, t)
-        return remote(spot, spot, gs_send.at[r, s], gs_recv.at[r, s], {"tp": sibling})
+        return remote(spot, spot, gs_send, gs_recv.at[r], {"tp": sibling})
 
     def pass_sibling(r, s, t):
         spot = grad_spot(r, s, t)
-        return remote(spot, spot, gf_send.at[r, s], gf_recv.at[r, s], {"tp": sibling})
-
-    def hop(r, ch, inward):
+        return remote(spot, spot, gf_send, gf_recv.at[r], {"tp": sibling})
+
+    def hop(r, ch, inward, slot):
         spot = held.at[rows_of(r, fsdp), ch.cols]
         to = inner if inward else edge
-        return remote(spot, spot, (z_in if inward else z_out).at[r], z_recv.at[r, ch.index], {"rep": to})
-
-    def hop_got(r, ch):
-        spot = held.at[rows_of(r, fsdp), ch.cols]
-        return remote(spot, spot, z_in.at[r], z_recv.at[r, ch.index], {"rep": inner})
+        return remote(spot, spot, z_in if inward else z_out, z_recv.at[slot, ch.index], {"rep": to})
+
+    def hop_got(slot, ch):
+        spot = held.at[pl.ds(0, rows), ch.cols]
+        return remote(spot, spot, z_in, z_recv.at[slot, ch.index], {"rep": inner})
 
     def hop_other(ch):
         spot = held.at[rows_of(edge, other), ch.cols]
-        return remote(spot, spot, zo_send, zo_recv.at[ch.index], {"rep": inner})
-
-    def cross(r, ch):
+        return remote(spot, spot, zo_send, x_recv.at[edge, ch.index], {"rep": inner})
+
+    def cross(r, ch, send=None):
         spot = held.at[rows_of(r, fsdp), ch.cols]
-        return remote(spot, spot, x_send.at[r], x_recv.at[r, ch.index], {"fsdp": other})
+        return remote(spot, spot, x_send if send is None else send, x_recv.at[r, ch.index], {"fsdp": other})
 
     def crossed(r, ch):
         spot = held.at[rows_of(r, other), ch.cols]
-        return remote(spot, spot, x_send.at[r], x_recv.at[r, ch.index], {"fsdp": other})
+        return remote(spot, spot, x_send, x_recv.at[r, ch.index], {"fsdp": other})
 
     def hop_extra(ch):
         spot = held.at[rows_of(near, other), ch.cols]
-        return remote(spot, spot, ze_send, ze_recv.at[ch.index], {"rep": jnp.where(is_edge, near, edge)})
-
-    def all_sent(r, s, width, send):
-        spot = held.at[rows_of(r, s), pl.ds(0, width)]
+        return remote(spot, spot, ze_send, x_recv.at[near, ch.index], {"rep": jnp.where(is_edge, near, edge)})
+
+    def all_sent(blocks, width, send):
+        spot = held.at[pl.ds(0, blocks * rows), pl.ds(0, width)]
         remote(spot, spot, send, gx_recv, {"fsdp": other}).wait_send()
 
     def when_extra(ch, act, otherwise):
         if isinstance(ch.index, int):
             act() if ch.index in extras else otherwise()
             return
-        pl.when(ch.index >= extras[0])(act)
-        pl.when(ch.index < extras[0])(otherwise)
+        pl.when(ch.index == extras[0])(act)
+        pl.when(ch.index != extras[0])(otherwise)
 
     def on_edge(act):
         pl.when(is_edge)(act)
@@ -201,8 +202,12 @@
 
     chunks_from(0, count, lambda ch: cross(rep, ch).start())
     early = 2
-    chunks_from(0, early, lambda ch: hop(rep, ch, True).start())
-    on_middle(lambda: chunks_from(0, early, lambda ch: hop(rep, ch, False).start()))
+
+    def own_inward(ch):
+        hop(rep, ch, True, jnp.where(is_edge, 0, 1)).start()
+
+    chunks_from(0, early, own_inward)
+    on_middle(lambda: chunks_from(0, early, lambda ch: hop(rep, ch, False, 0).start()))
 
     def share(r, s):
         over_y(r, s, tp).start()
@@ -212,9 +217,10 @@
         over_y(r, s, opposite).wait_recv()
         pass_sibling(r, s, opposite).start()
 
-    def settle(r, s):
-        to_sibling(r, s, sibling).wait_recv()
-        pass_sibling(r, s, past).wait_recv()
+    def settle(r, pairs):
+        spots = grads.at[pl.ds(0, pairs * rows), pl.ds(0, quarter)]
+        remote(spots, spots, gs_send, gs_recv.at[r], {"tp": sibling}).wait_recv()
+        remote(spots, spots, gf_send, gf_recv.at[r], {"tp": sibling}).wait_recv()
 
     tile = 256
 
@@ -237,25 +243,18 @@
             with jax.named_scope(f"{name}{at}"):
                 acts[name](*args)
 
-    def sent_shares(r, s):
-        over_y(r, s, tp).wait_send()
-        to_sibling(r, s, tp).wait_send()
-        pass_sibling(r, s, opposite).wait_send()
-
-    def sent_first():
+    def grads_sent(blocks, send):
+        all_sent(1, blocks * quarter, send)
+
+    def shares_sent():
         grad_across().wait_send()
-        sent_shares(rep, other)
-        grad_hop(rep, fsdp, True).wait_send()
-        grad_hop(rep, other, True).wait_send()
-        all_sent(rep, fsdp, columns, x_send.at[rep])
-        all_sent(rep, fsdp, columns, z_in.at[rep])
+        for send in (gy_send, gs_send, gf_send):
+            grads_sent(7, send)
 
     def clear():
         sums[fsdp * n_tp + tp] = jnp.zeros(sums.shape[1:], sums.dtype)
 
-    def multiply_tile(ch, m, squared):
-        spot = pl.ds(pl.multiple_of(m * TILE, TILE), TILE)
-        product = jnp.dot(turned[spot, :], held[:, ch.cols], preferred_element_type=jnp.float32)
+    def leave(product, spot, ch, squared):
         out_ref[spot, ch.cols] = product.astype(out_ref.dtype)
         if squared:
             squares = jnp.sum((product * product).reshape(TILE // 8, 8, ch.size), axis=0)
@@ -264,6 +263,38 @@
                 total = total + squares[:, at:at + LANES]
             sums[fsdp * n_tp + tp] += total
 
+    def tile_of(m):
+        return pl.ds(pl.multiple_of(m * TILE, TILE), TILE)
+
+    def multiply_tile(ch, m, squared):
+        spot = tile_of(m)
+        product = jnp.dot(turned[spot, :], held[:, ch.cols], preferred_element_type=jnp.float32)
+        leave(product, spot, ch, squared)
+
+    pair = 2 * rows
+    ends = {"first": pl.multiple_of(edge * pair, pair), "late": pl.multiple_of(far_edge * pair, pair)}
+
+    def part(spot, ch, start, size):
+        tokens = pl.ds(start, size)
+        return jnp.dot(turned[spot, tokens], held[tokens, ch.cols], preferred_element_type=jnp.float32)
+
+    def kept(ch):
+        return pl.ds((ch.index - (count - 2)) * WIDTH, ch.size)
+
+    def begin(ch):
+        @pl.loop(0, tiles)
+        def _(m):
+            spot = tile_of(m)
+            middle_part[spot, kept(ch)] = part(spot, ch, pair, 2 * pair)
+            end_part[spot, kept(ch)] = part(spot, ch, ends["first"], pair)
+
+    def complete(ch, squared):
+        @pl.loop(0, tiles)
+        def _(m):
+            spot = tile_of(m)
+            both = end_part[spot, kept(ch)] + part(spot, ch, ends["late"], pair)
+            leave(middle_part[spot, kept(ch)] + both, spot, ch, squared)
+
     tiles = half // TILE
 
     def finish(ch, arrived, squared):
@@ -272,10 +303,14 @@
         with jax.named_scope("multiply_last"):
             pl.loop(0, tiles)(lambda m: multiply_tile(ch, m, squared))
 
-    def sweep(events, arrived, between, ended, lag, squared):
+    def sweep(events, arrived_but_last, between, ended, lag, squared):
+        def arrived(ch):
+            arrived_but_last(ch)
+            crossed(far_edge, ch).wait_recv()
+
         places = [at * tiles // len(events) for at in range(len(events))]
 
-        def step(index):
+        def step(index, events=events):
             ch, lagging = chunk(index), chunk(index - lag)
             with jax.named_scope("arrived"):
                 arrived(lagging)
@@ -290,12 +325,22 @@
                 with jax.named_scope("multiply"):
                     multiply_tile(lagging, m, squared)
 
-        pl.loop(LAG, full - 1)(step)
+        pl.loop(LAG, count - 2)(step)
         between()
-        for index in range(full - 1, count):
-            step(index)
+        ahead, far_pull, last_pull = events
+        last_two = chunk(count - 2), chunk(count - 1)
+        for at, pull in ((0, far_pull), (1, last_pull)):
+            step(count - 2 + at, [lambda ch: ahead(ch), lambda ch: pull(last_two[0]), lambda ch: pull(last_two[1])])
         ended()
-        chunks_from(count - lag, count, lambda ch: finish(ch, arrived, squared))
+        chunks_from(count - lag, count - 2, lambda ch: finish(ch, arrived, squared))
+        for ch in last_two:
+            with jax.named_scope("begin"):
+                arrived_but_last(ch)
+                begin(ch)
+        for ch in last_two:
+            with jax.named_scope("late"):
+                crossed(far_edge, ch).wait_recv()
+                complete(ch, squared)
 
     @on_edge
     def _():
@@ -309,34 +354,29 @@
         def land(name, s, whole):
             r = rep if name == "rep" else places[name]
             pass_on(r, sides[s])
-            settle_later.append((r, sides[s]))
             if whole:
-                for pair in settle_later:
-                    settle(*pair)
-                settle_later.clear()
+                settle(r, 1 if name == "rep" else 2)
                 turn(r)
-
-        settle_later = []
 
         def relay(*indices):
             for index in indices:
                 if index + early < count:
-                    hop(rep, chunk(index + early), True).start()
+                    own_inward(chunk(index + early))
                 if index < count:
                     crossed(edge, chunk(index)).wait_recv()
                     hop_other(chunk(index)).start()
 
-        def pull(r):
+        def pull(slot, r):
             def event(ch):
-                hop_got(r, ch).wait_recv()
+                hop_got(slot, ch).wait_recv()
                 cross(r, ch).start()
             return event
 
         def pull_near(ch):
-            hop_got(near, ch).wait_recv()
-            when_extra(ch, lambda: None, lambda: cross(near, ch).start())
-
-        pulls = [pull(far), pull(far_edge)]
+            hop_got(0, ch).wait_recv()
+            when_extra(ch, lambda: None, lambda: cross(near, ch, xn_send).start())
+
+        pulls = [pull(1, far), pull(2, far_edge)]
 
         def near_at(*indices):
             for index in indices:
@@ -360,14 +400,14 @@
                     event(chunk(index))
 
         def arrived(ch):
-            when_extra(
-                ch, lambda: hop_extra(ch).wait_recv(), lambda: crossed(near, ch).wait_recv()
-            )
-            for r in (far, far_edge):
-                crossed(r, ch).wait_recv()
+            crossed(near, ch).wait_recv()
+            crossed(far, ch).wait_recv()
 
         def compute(index):
-            finish(chunk(index), arrived, False)
+            def whole(ch):
+                arrived(ch)
+                crossed(far_edge, ch).wait_recv()
+            finish(chunk(index), whole, False)
 
         def batch(k):
             return range(k * count // 8, (k + 1) * count // 8)
@@ -390,16 +430,14 @@
         )
 
         def between():
-            sent_first()
-            for r in (near, far, far_edge):
-                for s in (fsdp, other):
-                    sent_shares(r, s)
-            all_sent(rep, other, columns, zo_send)
+            shares_sent()
+            grads_sent(2, gz_in)
+            all_sent(1, columns, z_in)
+            all_sent(1, columns, zo_send)
 
         sweep([near_ahead, *pulls], arrived, between, lambda: None, EDGE_LAG, False)
-        all_sent(near, fsdp, columns - extra_columns, x_send.at[near])
-        for r in (far, far_edge):
-            all_sent(r, fsdp, columns, x_send.at[r])
+        all_sent(1, columns - extra_columns, xn_send)
+        all_sent(3, columns, x_send)
 
     @on_middle
     def _():
@@ -412,28 +450,24 @@
             grad_hop(r, s, name == "edge").start()
             share(r, s)
 
-        settle_later = {}
-
-        def land(name, s):
+        def land(name, s, whole=True):
             r = rep if name == "rep" else places[name]
             pass_on(r, sides[s])
-            settle_later.setdefault(name, []).append((r, sides[s]))
-            if len(settle_later[name]) == (1 if name == "rep" else 2):
-                for pair in settle_later[name]:
-                    settle(*pair)
+            if whole:
+                settle(r, 1 if name == "rep" else 2)
                 turn(r)
 
         def inward(*indices):
             for index in indices:
                 ch = chunk(index)
                 if not isinstance(index, int) or index >= early:
-                    hop(rep, ch, True).start()
-                hop_got(edge, ch).wait_recv()
-                hop(edge, ch, True).start()
+                    own_inward(ch)
+                hop_got(0, ch).wait_recv()
+                hop(edge, ch, True, 2).start()
 
         def fill(*indices):
             for index in indices:
-                hop(rep, chunk(index), False).start()
+                hop(rep, chunk(index), False, 0).start()
 
         def outer(ch):
             if isinstance(ch.index, int):
@@ -444,6 +478,12 @@
                 if full < count:
                     pl.when(ch.index + FILL == full)(lambda: fill(full))
             follow(ch.index + AHEAD)
+            if not isinstance(ch.index, int):
+                pl.when(ch.index == EXTRA)(lambda: send_extra(ch))
+
+        def send_extra(ch):
+            crossed(rep, ch).wait_recv()
+            hop_extra(ch).start()
 
         def follow(index):
             if isinstance(index, int):
@@ -454,14 +494,14 @@
             if full < count:
                 pl.when(index == full)(lambda: inward(full))
 
-        def pull(r):
+        def pull(slot, r):
             def event(ch):
-                hop_got(r, ch).wait_recv()
-                hop(r, ch, False).start()
+                hop_got(slot, ch).wait_recv()
+                hop(r, ch, False, slot).start()
                 cross(r, ch).start()
             return event
 
-        pulls = [pull(far), pull(far_edge)]
+        pulls = [pull(1, far), pull(2, far_edge)]
 
         def early_events(*indices):
             for index in indices:
@@ -475,10 +515,10 @@
                 ("own",), ("take", "far", "own"), ("fill", early), ("take", "edge", "own"),
                 ("take", "edge", "other"), ("inward", *range(early)), ("take", "far", "other"),
                 ("fill", early + 1), ("land", "rep", "other"), ("take", "last", "own"),
-                ("fill", early + 2), ("land", "far", "own"),
-                ("inward", *range(early, LAG)), ("take", "last", "other"), ("land", "edge", "own"),
+                ("fill", early + 2), ("land", "far", "own", False),
+                ("inward", *range(early, LAG)), ("take", "last", "other"), ("land", "edge", "own", False),
                 ("early", 0, 1), ("inward", *range(LAG, LAG + 2)), ("land", "edge", "other"),
-                ("land", "far", "other"), ("early", 2), ("inward", LAG + 2), ("land", "last", "own"),
+                ("land", "far", "other"), ("early", 2), ("inward", LAG + 2), ("land", "last", "own", False),
                 ("early", 3), ("inward", LAG + 3), ("land", "last", "other"),
             ],
             {"own": take_own, "take": take, "land": land, "inward": inward, "early": early_events, "fill": fill},
@@ -487,38 +527,34 @@
         def arrived(ch):
             hop_other(ch).wait_recv()
             when_extra(ch, lambda: None, lambda: crossed(rep, ch).wait_recv())
-            for r in (far, far_edge):
-                crossed(r, ch).wait_recv()
+            crossed(far, ch).wait_recv()
 
         clear()
 
         def ended():
-            for index in extras:
-                crossed(rep, chunk(index)).wait_recv()
-                hop_extra(chunk(index)).start()
+            send_extra(chunk(count - 1))
 
         sweep([outer, *pulls], arrived, lambda: None, ended, LAG, True)
 
         mine = fsdp * n_tp + tp
         peers = [(a, k) for a in range(2) for k in range(n_tp) if a or k]
 
-        def exchange(at, towards):
+        def exchange(at):
             a, k = peers[at]
             to_side = other if a else fsdp
-            to_tp = lax.rem(tp + (k if towards else n_tp - k), n_tp)
-            spot = sums.at[mine if towards else to_side * n_tp + to_tp]
-            return remote(spot, spot, sq_send.at[at], sq_recv.at[at], {"fsdp": to_side, "tp": to_tp})
+            to_tp = lax.rem(tp + k, n_tp)
+            spot = sums.at[mine]
+            return remote(spot, spot, sq_send, sq_recv, {"fsdp": to_side, "tp": to_tp})
 
         for at in range(len(peers)):
-            exchange(at, True).start()
+            exchange(at).start()
         with jax.named_scope("exchange"):
-            for at in range(len(peers)):
-                exchange(at, False).wait_recv()
+            seven = sums.at[pl.ds(0, len(peers))]
+            remote(seven, seven, sq_send, sq_recv, {"fsdp": other}).wait_recv()
         square_total = jnp.sum(jnp.sum(sums[...], axis=0), keepdims=True)
         factor = 1.0 / jnp.sqrt(square_total / entry_count + 1e-06)
         total_out[...] = jnp.broadcast_to(factor, total_out.shape)
-        for at in range(len(peers)):
-            exchange(at, True).wait_send()
+        remote(seven, seven, sq_send, sq_recv, {"fsdp": other}).wait_send()
 
     def tell():
         return remote(total_out, total_out, fa_send, fa_recv, {"rep": jnp.where(is_edge, near, edge)})
@@ -531,20 +567,13 @@
     @on_middle
     def _():
         tell().wait_send()
-        sent_first()
-        for s in (fsdp, other):
-            grad_hop(rep, s, False).wait_send()
-            grad_hop(edge, s, True).wait_send()
-            for r in (edge, far, far_edge):
-                sent_shares(r, s)
-            for r in (far, far_edge):
-                grad_hop(r, s, False).wait_send()
-        all_sent(edge, fsdp, columns, z_in.at[edge])
-        for r in (rep, far, far_edge):
-            all_sent(r, fsdp, columns, z_out.at[r])
-        for r in (far, far_edge):
-            all_sent(r, fsdp, columns, x_send.at[r])
-        all_sent(rep, other, extra_columns, ze_send)
+        shares_sent()
+        grads_sent(4, gz_in)
+        grads_sent(6, gz_out)
+        all_sent(2, columns, z_in)
+        all_sent(3, columns, z_out)
+        all_sent(3, columns, x_send)
+        all_sent(1, extra_columns, ze_send)
 
 
 def by_kernel(n_rep, n_tp, entry_count, gate_pre, up_pre, out_grad):
@@ -554,8 +583,7 @@
     quarter = half // n_tp
     count = chunking(columns)[1]
     dma = pltpu.SemaphoreType.DMA
-    block, piece, line = dma((n_rep, 2)), dma((n_rep, count)), dma((count,))
-    whole = dma((n_rep,))
+    block, whole = dma((n_rep, 2)), dma((n_rep,))
     return pl.pallas_call(
         functools.partial(gather_multiply, entry_count),
         out_shape=(
@@ -573,10 +601,12 @@
             pltpu.VMEM((rows, quarter), jnp.bfloat16),
             pltpu.VMEM((2 * n_tp, 8, LANES), jnp.float32),
             pltpu.VMEM((8, LANES), jnp.float32),
-            dma((4,)), dma, dma, block, block, block, block, block,
-            block, block, block, block,
-            piece, whole, whole, line, dma, line, dma, whole, piece,
-            dma((2 * n_tp - 1,)), dma((2 * n_tp - 1,)), dma, dma,
+            pltpu.VMEM((half, 2 * WIDTH), jnp.float32),
+            pltpu.VMEM((half, 2 * WIDTH), jnp.float32),
+            dma((4,)), dma, dma, block, dma, dma, dma, block,
+            dma, whole, dma, whole,
+            dma((3, count)), dma, dma, dma, dma, dma, dma, dma((n_rep, count)),
+            dma, dma, dma, dma,
         ],
         compiler_params=pltpu.CompilerParams(
             collective_id=0, has_side_effects=True, vmem_limit_bytes=VMEM_LIMIT * 3 // 4
@@ -641,8 +671,9 @@
 def kernel_fits(n_rep, n_fsdp, n_tp, rows, columns, features):
     tokens, half = rows * n_rep * n_fsdp, features // n_fsdp
     held_bytes = 2 * (tokens * columns + 2 * tokens * half + half * columns + 2 * rows * columns)
+    held_bytes += 16 * half * WIDTH
     aligned = rows % 128 == 0 and columns % LANES == 0 and half % (LANES * n_tp) == 0
-    shaped = (n_rep, n_fsdp, n_tp) == (4, 2, 4) and columns >= 12 * WIDTH
+    shaped = (n_rep, n_fsdp, n_tp) == (4, 2, 4) and columns >= max(12 * WIDTH, 7 * half // n_tp)
     return shaped and aligned and half % TILE == 0 and held_bytes < VMEM_LIMIT * 3 // 4
 
 

time: 98.3 us -> 98.5 us (level)
  no operation moved by 1% of the time
where the time goes in v5:
time: 98.5 us; the launch traced here: 98.3 us
  Pallas kernels  98.3 us (100%)
    pallas_call x1, Pallas kernels, by_kernel(): pl.pallas_call(functools.partial(gather_multiply, entry_count), out_shape...  92.7 us
    pallas_call x1, Pallas kernels, scale(): pl.pallas_call(body, out_shape=jax.ShapeDtypeStruct((half, columns), jnp....  5.58 us

profile of v5, /device:TPU:0, one launch (start us, length us, event | category | flops | bytes accessed | tf_op | source)
XLA Modules:
  0.0 98.3 jit_solution(12998692148114465428)
XLA Ops:
  0.0 92.7 %shard_map.37 = (bf16[2048,3712]{1,0:T(8,128)(2,1)S(1)}, f32[8,128]{1,0:T(8,128)S(1)}) custom-call(bf16[128,3712]{1,0:T(8,128)(2,1)} %gate_ref.1, bf16[128,3712]{1,0:T(8,128)(2,1)} %up_ref.1, bf16[128,4096]{1,0:T(8,128)(2,1)} %grad_ref.1), custom_call_target="tpu_custom_call" | custom-call | tf_op jit(solution)/shard_map/pallas_call | solution.py:587
  92.8 5.6 %shard_map.38 = bf16[2048,3712]{1,0:T(8,128)(2,1)} custom-call(bf16[2048,3712]{1,0:T(8,128)(2,1)S(1)} %get-tuple-element.7.summed_ref, f32[8,128]{1,0:T(8,128)S(1)} %get-tuple-element.8.factor_ref), custom_call_target="tpu_custom_call" | custom-call | tf_op jit(solution)/shard_map/pallas_call | solution.py:648

commit v6 on v5

--- a/solution.py
+++ b/solution.py
@@ -16,7 +16,7 @@
 EDGE_LAG = 2
 AHEAD = 4
 FILL = 3
-EXTRA = 8
+EXTRA = (5, 9)
 
 
 class Chunk:
@@ -57,8 +57,8 @@
     n_tp = 4
     quarter = half // n_tp
     full, count, chunk = chunking(columns)
-    extras = (EXTRA, count - 1)
-    extra_columns = WIDTH + chunk(count - 1).size
+    extras = (*EXTRA, count - 1)
+    extra_columns = len(EXTRA) * WIDTH + chunk(count - 1).size
     other = 1 - fsdp
     side = rep // 2
     edge, near, far, far_edge = 3 * side, 1 + side, 2 - side, 3 - 3 * side
@@ -175,12 +175,15 @@
         spot = held.at[pl.ds(0, blocks * rows), pl.ds(0, width)]
         remote(spot, spot, send, gx_recv, {"fsdp": other}).wait_send()
 
+    def among_extra(index):
+        return functools.reduce(jnp.logical_or, [index == at for at in EXTRA])
+
     def when_extra(ch, act, otherwise):
         if isinstance(ch.index, int):
             act() if ch.index in extras else otherwise()
             return
-        pl.when(ch.index == extras[0])(act)
-        pl.when(ch.index != extras[0])(otherwise)
+        pl.when(among_extra(ch.index))(act)
+        pl.when(jnp.logical_not(among_extra(ch.index)))(otherwise)
 
     def on_edge(act):
         pl.when(is_edge)(act)
@@ -286,6 +289,11 @@
         def _(m):
             spot = tile_of(m)
             middle_part[spot, kept(ch)] = part(spot, ch, pair, 2 * pair)
+
+    def begin_end(ch):
+        @pl.loop(0, tiles)
+        def _(m):
+            spot = tile_of(m)
             end_part[spot, kept(ch)] = part(spot, ch, ends["first"], pair)
 
     def complete(ch, squared):
@@ -337,6 +345,8 @@
             with jax.named_scope("begin"):
                 arrived_but_last(ch)
                 begin(ch)
+                if squared:
+                    begin_end(ch)
         for ch in last_two:
             with jax.named_scope("late"):
                 crossed(far_edge, ch).wait_recv()
@@ -434,6 +444,8 @@
             grads_sent(2, gz_in)
             all_sent(1, columns, z_in)
             all_sent(1, columns, zo_send)
+            for index in (count - 2, count - 1):
+                begin_end(chunk(index))
 
         sweep([near_ahead, *pulls], arrived, between, lambda: None, EDGE_LAG, False)
         all_sent(1, columns - extra_columns, xn_send)
@@ -479,7 +491,7 @@
                     pl.when(ch.index + FILL == full)(lambda: fill(full))
             follow(ch.index + AHEAD)
             if not isinstance(ch.index, int):
-                pl.when(ch.index == EXTRA)(lambda: send_extra(ch))
+                pl.when(among_extra(ch.index))(lambda: send_extra(ch))
 
         def send_extra(ch):
             crossed(rep, ch).wait_recv()

time: 98.5 us -> 99.6 us (1.011)
  Pallas kernels: 98.3 us -> 99.5 us
    pallas_call x1, Pallas kernels: 92.7 us -> 93.9 us  [by_kernel(): pl.pallas_call(functools.partial(gather_multiply, entry_count), out_shape...]
where the time goes in v6:
time: 99.6 us; the launch traced here: 99.5 us
  Pallas kernels  99.5 us (100%)
    pallas_call x1, Pallas kernels, by_kernel(): pl.pallas_call(functools.partial(gather_multiply, entry_count), out_shape...  93.9 us
    pallas_call x1, Pallas kernels, scale(): pl.pallas_call(body, out_shape=jax.ShapeDtypeStruct((half, columns), jnp....  5.58 us

profile of v6, /device:TPU:0, one launch (start us, length us, event | category | flops | bytes accessed | tf_op | source)
XLA Modules:
  0.0 99.5 jit_solution(12459255428509449606)
XLA Ops:
  0.0 93.9 %shard_map.37 = (bf16[2048,3712]{1,0:T(8,128)(2,1)S(1)}, f32[8,128]{1,0:T(8,128)S(1)}) custom-call(bf16[128,3712]{1,0:T(8,128)(2,1)} %gate_ref.1, bf16[128,3712]{1,0:T(8,128)(2,1)} %up_ref.1, bf16[128,4096]{1,0:T(8,128)(2,1)} %grad_ref.1), custom_call_target="tpu_custom_call" | custom-call | tf_op jit(solution)/shard_map/pallas_call | solution.py:599
  93.9 5.6 %shard_map.38 = bf16[2048,3712]{1,0:T(8,128)(2,1)} custom-call(bf16[2048,3712]{1,0:T(8,128)(2,1)S(1)} %get-tuple-element.7.summed_ref, f32[8,128]{1,0:T(8,128)S(1)} %get-tuple-element.8.factor_ref), custom_call_target="tpu_custom_call" | custom-call | tf_op jit(solution)/shard_map/pallas_call | solution.py:660

commit v7 on v6

--- a/solution.py
+++ b/solution.py
@@ -16,7 +16,7 @@
 EDGE_LAG = 2
 AHEAD = 4
 FILL = 3
-EXTRA = (5, 9)
+EXTRA = (8,)
 
 
 class Chunk:
@@ -318,17 +318,17 @@
 
         places = [at * tiles // len(events) for at in range(len(events))]
 
-        def step(index, events=events):
+        def step(index):
             ch, lagging = chunk(index), chunk(index - lag)
-            with jax.named_scope("arrived"):
-                arrived(lagging)
+            plan = [(place, event, ch) for place, event in zip(places, events)]
+            plan.insert(sum(place == 0 for place in places), (0, arrived, lagging))
 
             @pl.loop(0, tiles)
             def _(m):
-                for at, (place, event) in enumerate(zip(places, events)):
+                for at, (place, event, subject) in enumerate(plan):
                     def run():
                         with jax.named_scope(f"event{at}"):
-                            event(ch)
+                            event(subject)
                     pl.when(m == place)(run)
                 with jax.named_scope("multiply"):
                     multiply_tile(lagging, m, squared)
@@ -337,8 +337,12 @@
         between()
         ahead, far_pull, last_pull = events
         last_two = chunk(count - 2), chunk(count - 1)
-        for at, pull in ((0, far_pull), (1, last_pull)):
-            step(count - 2 + at, [lambda ch: ahead(ch), lambda ch: pull(last_two[0]), lambda ch: pull(last_two[1])])
+        for index, pull in ((count - 2, far_pull), (count - 1, last_pull)):
+            with jax.named_scope("pull_last"):
+                ahead(chunk(index))
+                for ch in last_two:
+                    pull(ch)
+            finish(chunk(index - lag), arrived, squared)
         ended()
         chunks_from(count - lag, count - 2, lambda ch: finish(ch, arrived, squared))
         for ch in last_two:

time: 99.6 us -> 98.2 us (0.986)
  Pallas kernels: 99.5 us -> 98.1 us
    pallas_call x1, Pallas kernels: 93.9 us -> 92.5 us  [by_kernel(): pl.pallas_call(functools.partial(gather_multiply, entry_count), out_shape...]
where the time goes in v7:
time: 98.2 us; the launch traced here: 98.1 us
  Pallas kernels  98.1 us (100%)
    pallas_call x1, Pallas kernels, by_kernel(): pl.pallas_call(functools.partial(gather_multiply, entry_count), out_shape...  92.5 us
    pallas_call x1, Pallas kernels, scale(): pl.pallas_call(body, out_shape=jax.ShapeDtypeStruct((half, columns), jnp....  5.58 us

profile of v7, /device:TPU:0, one launch (start us, length us, event | category | flops | bytes accessed | tf_op | source)
XLA Modules:
  0.0 98.1 jit_solution(4367567559019398794)
XLA Ops:
  0.0 92.5 %shard_map.37 = (bf16[2048,3712]{1,0:T(8,128)(2,1)S(1)}, f32[8,128]{1,0:T(8,128)S(1)}) custom-call(bf16[128,3712]{1,0:T(8,128)(2,1)} %gate_ref.1, bf16[128,3712]{1,0:T(8,128)(2,1)} %up_ref.1, bf16[128,4096]{1,0:T(8,128)(2,1)} %grad_ref.1), custom_call_target="tpu_custom_call" | custom-call | tf_op jit(solution)/shard_map/pallas_call | solution.py:603
  92.5 5.6 %shard_map.38 = bf16[2048,3712]{1,0:T(8,128)(2,1)} custom-call(bf16[2048,3712]{1,0:T(8,128)(2,1)S(1)} %get-tuple-element.7.summed_ref, f32[8,128]{1,0:T(8,128)S(1)} %get-tuple-element.8.factor_ref), custom_call_target="tpu_custom_call" | custom-call | tf_op jit(solution)/shard_map/pallas_call | solution.py:664

commit v8 on v7

--- a/solution.py
+++ b/solution.py
@@ -203,7 +203,6 @@
     grad_hop(rep, fsdp, True).start()
     on_middle(lambda: grad_hop(rep, fsdp, False).start())
 
-    chunks_from(0, count, lambda ch: cross(rep, ch).start())
     early = 2
 
     def own_inward(ch):
@@ -211,6 +210,12 @@
 
     chunks_from(0, early, own_inward)
     on_middle(lambda: chunks_from(0, early, lambda ch: hop(rep, ch, False, 0).start()))
+
+    def own_across(low, high):
+        for index in range(low, min(high, count)):
+            cross(rep, chunk(index)).start()
+
+    own_across(0, 4)
 
     def share(r, s):
         over_y(r, s, tp).start()
@@ -428,9 +433,10 @@
 
         perform(
             [
-                ("own",), ("take", "near", "own"), ("relay", *batch(0)), ("near", *range(early)),
-                ("take", "near", "other"), ("land", "rep", "other", True), ("relay", *batch(1)),
-                ("take", "far", "own"), ("near", early), ("land", "near", "own", False),
+                ("own",), ("across", 4, 9), ("take", "near", "own"), ("relay", *batch(0)),
+                ("near", *range(early)), ("take", "near", "other"), ("across", 9, 12),
+                ("land", "rep", "other", True), ("relay", *batch(1)),
+                ("take", "far", "own"), ("across", 12, count), ("near", early), ("land", "near", "own", False),
                 ("relay", *batch(2)), ("take", "far", "other"), ("near", early + 1),
                 ("land", "near", "other", True), ("relay", *batch(3)), ("take", "last", "own"),
                 ("near", early + 2), ("land", "far", "own", False), ("relay", *batch(4)),
@@ -440,7 +446,7 @@
                 ("compute", 0), ("early", 3), ("compute", 1),
             ],
             {"own": take_own, "take": take, "land": land, "relay": relay, "early": early_events, "near": near_at,
-             "compute": compute},
+             "compute": compute, "across": own_across},
         )
 
         def between():
@@ -528,16 +534,19 @@
 
         perform(
             [
-                ("own",), ("take", "far", "own"), ("fill", early), ("take", "edge", "own"),
-                ("take", "edge", "other"), ("inward", *range(early)), ("take", "far", "other"),
+                ("own",), ("take", "far", "own"), ("across", 4, 9), ("fill", early),
+                ("take", "edge", "own"), ("take", "edge", "other"), ("across", 9, 12),
+                ("inward", *range(early)), ("take", "far", "other"),
                 ("fill", early + 1), ("land", "rep", "other"), ("take", "last", "own"),
+                ("across", 12, count),
                 ("fill", early + 2), ("land", "far", "own", False),
                 ("inward", *range(early, LAG)), ("take", "last", "other"), ("land", "edge", "own", False),
                 ("early", 0, 1), ("inward", *range(LAG, LAG + 2)), ("land", "edge", "other"),
                 ("land", "far", "other"), ("early", 2), ("inward", LAG + 2), ("land", "last", "own", False),
                 ("early", 3), ("inward", LAG + 3), ("land", "last", "other"),
             ],
-            {"own": take_own, "take": take, "land": land, "inward": inward, "early": early_events, "fill": fill},
+            {"own": take_own, "take": take, "land": land, "inward": inward, "early": early_events, "fill": fill,
+             "across": own_across},
         )
 
         def arrived(ch):

time: 98.2 us -> 98.2 us (level)
  no operation moved by 1% of the time
where the time goes in v8:
time: 98.2 us; the launch traced here: 98.1 us
  Pallas kernels  98.1 us (100%)
    pallas_call x1, Pallas kernels, by_kernel(): pl.pallas_call(functools.partial(gather_multiply, entry_count), out_shape...  92.5 us
    pallas_call x1, Pallas kernels, scale(): pl.pallas_call(body, out_shape=jax.ShapeDtypeStruct((half, columns), jnp....  5.58 us

profile of v8, /device:TPU:0, one launch (start us, length us, event | category | flops | bytes accessed | tf_op | source)
XLA Modules:
  0.0 98.1 jit_solution(5212760506908197676)
XLA Ops:
  0.0 92.5 %shard_map.37 = (bf16[2048,3712]{1,0:T(8,128)(2,1)S(1)}, f32[8,128]{1,0:T(8,128)S(1)}) custom-call(bf16[128,3712]{1,0:T(8,128)(2,1)} %gate_ref.1, bf16[128,3712]{1,0:T(8,128)(2,1)} %up_ref.1, bf16[128,4096]{1,0:T(8,128)(2,1)} %grad_ref.1), custom_call_target="tpu_custom_call" | custom-call | tf_op jit(solution)/shard_map/pallas_call | solution.py:612
  92.5 5.6 %shard_map.38 = bf16[2048,3712]{1,0:T(8,128)(2,1)} custom-call(bf16[2048,3712]{1,0:T(8,128)(2,1)S(1)} %get-tuple-element.7.summed_ref, f32[8,128]{1,0:T(8,128)S(1)} %get-tuple-element.8.factor_ref), custom_call_target="tpu_custom_call" | custom-call | tf_op jit(solution)/shard_map/pallas_call | solution.py:673

commit v9 on v8

--- a/solution.py
+++ b/solution.py
@@ -16,7 +16,7 @@
 EDGE_LAG = 2
 AHEAD = 4
 FILL = 3
-EXTRA = (8,)
+EXTRA = (5, 9)
 
 
 class Chunk:
@@ -81,16 +81,16 @@
         )
 
     loads = [
-        pltpu.make_async_copy(gate_ref, gate_in, local_sem.at[0]),
-        pltpu.make_async_copy(up_ref, up_in, local_sem.at[1]),
+        pltpu.make_async_copy(
+            grad_ref.at[:, pl.ds(pl.multiple_of(other * half + tp * quarter, LANES), quarter)],
+            across_in, local_sem.at[0],
+        ),
         pltpu.make_async_copy(
             grad_ref.at[:, pl.ds(pl.multiple_of(fsdp * half, LANES), half)],
-            grads.at[rows_of(rep, fsdp), :], local_sem.at[2],
+            grads.at[rows_of(rep, fsdp), :], local_sem.at[1],
         ),
-        pltpu.make_async_copy(
-            grad_ref.at[:, pl.ds(pl.multiple_of(other * half + tp * quarter, LANES), quarter)],
-            across_in, local_sem.at[3],
-        ),
+        pltpu.make_async_copy(gate_ref, gate_in, local_sem.at[2]),
+        pltpu.make_async_copy(up_ref, up_in, local_sem.at[3]),
     ]
     for load in loads:
         load.start()
@@ -104,9 +104,98 @@
     def _():
         pl.semaphore_signal(barrier, inc=1, device_id={"rep": edge}, device_id_type=MESH)
 
+    with jax.named_scope("barrier"):
+        pl.semaphore_wait(barrier, 4 + jnp.where(is_edge, 0, 1))
+
+    def grad_across():
+        return remote(across_in, grads.at[rows_of(rep, fsdp), quarter_of(tp)], gx_send, gx_recv, {"fsdp": other})
+
+    def grad_spot(r, s, t):
+        return grads.at[rows_of(r, s), quarter_of(t)]
+
+    def grad_hop(r, s, inward):
+        spot = grad_spot(r, s, tp)
+        to = inner if inward else edge
+        return remote(spot, spot, (gz_in if inward else gz_out), gz_recv.at[r, s], {"rep": to})
+
+    def grad_got(r, s):
+        spot = grad_spot(r, s, tp)
+        return remote(spot, spot, gz_in, gz_recv.at[r, s], {"rep": inner})
+
+    def over_y(r, s, t):
+        spot = grad_spot(r, s, t)
+        return remote(spot, spot, gy_send, gy_recv.at[r, s], {"tp": opposite})
+
+    def to_sibling(r, s, t):
+        spot = grad_spot(r, s, t)
+        return remote(spot, spot, gs_send, gs_recv.at[r], {"tp": sibling})
+
+    def pass_sibling(r, s, t):
+        spot = grad_spot(r, s, t)
+        return remote(spot, spot, gf_send, gf_recv.at[r], {"tp": sibling})
+
+    def hop(r, ch, inward, slot):
+        spot = held.at[rows_of(r, fsdp), ch.cols]
+        to = inner if inward else edge
+        return remote(spot, spot, z_in if inward else z_out, z_recv.at[slot, ch.index], {"rep": to})
+
+    def hop_got(slot, ch):
+        spot = held.at[pl.ds(0, rows), ch.cols]
+        return remote(spot, spot, z_in, z_recv.at[slot, ch.index], {"rep": inner})
+
+    def hop_other(ch):
+        spot = held.at[rows_of(edge, other), ch.cols]
+        return remote(spot, spot, zo_send, x_recv.at[edge, ch.index], {"rep": inner})
+
+    def cross(r, ch, send=None):
+        spot = held.at[rows_of(r, fsdp), ch.cols]
+        return remote(spot, spot, x_send if send is None else send, x_recv.at[r, ch.index], {"fsdp": other})
+
+    def crossed(r, ch):
+        spot = held.at[rows_of(r, other), ch.cols]
+        return remote(spot, spot, x_send, x_recv.at[r, ch.index], {"fsdp": other})
+
+    def hop_extra(ch):
+        spot = held.at[rows_of(near, other), ch.cols]
+        return remote(spot, spot, ze_send, x_recv.at[near, ch.index], {"rep": jnp.where(is_edge, near, edge)})
+
+    def all_sent(blocks, width, send):
+        spot = held.at[pl.ds(0, blocks * rows), pl.ds(0, width)]
+        remote(spot, spot, send, gx_recv, {"fsdp": other}).wait_send()
+
+    def among_extra(index):
+        return functools.reduce(jnp.logical_or, [index == at for at in EXTRA])
+
+    def when_extra(ch, act, otherwise):
+        if isinstance(ch.index, int):
+            act() if ch.index in extras else otherwise()
+            return
+        pl.when(among_extra(ch.index))(act)
+        pl.when(jnp.logical_not(among_extra(ch.index)))(otherwise)
+
+    def on_edge(act):
+        pl.when(is_edge)(act)
+
+    def on_middle(act):
+        pl.when(jnp.logical_not(is_edge))(act)
+
+    def chunks_from(low, high, act):
+        if low < min(high, full):
+            @pl.loop(low, min(high, full))
+            def _(index):
+                act(chunk(index))
+        if full < count == high:
+            act(chunk(full))
+
+    loads[0].wait()
+    grad_across().start()
+    loads[1].wait()
+    grad_hop(rep, fsdp, True).start()
+    on_middle(lambda: grad_hop(rep, fsdp, False).start())
+
     with jax.named_scope("load"):
-        for load in loads:
-            load.wait()
+        loads[2].wait()
+        loads[3].wait()
 
     @pl.loop(0, columns // LANES)
     def _(at):
@@ -115,93 +204,6 @@
         held[rows_of(rep, fsdp), cols] = (
             jax.nn.silu(gate) * up_in[:, cols].astype(jnp.float32)
         ).astype(held.dtype)
-
-    with jax.named_scope("barrier"):
-        pl.semaphore_wait(barrier, 4 + jnp.where(is_edge, 0, 1))
-
-    def grad_across():
-        return remote(across_in, grads.at[rows_of(rep, fsdp), quarter_of(tp)], gx_send, gx_recv, {"fsdp": other})
-
-    def grad_spot(r, s, t):
-        return grads.at[rows_of(r, s), quarter_of(t)]
-
-    def grad_hop(r, s, inward):
-        spot = grad_spot(r, s, tp)
-        to = inner if inward else edge
-        return remote(spot, spot, (gz_in if inward else gz_out), gz_recv.at[r, s], {"rep": to})
-
-    def grad_got(r, s):
-        spot = grad_spot(r, s, tp)
-        return remote(spot, spot, gz_in, gz_recv.at[r, s], {"rep": inner})
-
-    def over_y(r, s, t):
-        spot = grad_spot(r, s, t)
-        return remote(spot, spot, gy_send, gy_recv.at[r, s], {"tp": opposite})
-
-    def to_sibling(r, s, t):
-        spot = grad_spot(r, s, t)
-        return remote(spot, spot, gs_send, gs_recv.at[r], {"tp": sibling})
-
-    def pass_sibling(r, s, t):
-        spot = grad_spot(r, s, t)
-        return remote(spot, spot, gf_send, gf_recv.at[r], {"tp": sibling})
-
-    def hop(r, ch, inward, slot):
-        spot = held.at[rows_of(r, fsdp), ch.cols]
-        to = inner if inward else edge
-        return remote(spot, spot, z_in if inward else z_out, z_recv.at[slot, ch.index], {"rep": to})
-
-    def hop_got(slot, ch):
-        spot = held.at[pl.ds(0, rows), ch.cols]
-        return remote(spot, spot, z_in, z_recv.at[slot, ch.index], {"rep": inner})
-
-    def hop_other(ch):
-        spot = held.at[rows_of(edge, other), ch.cols]
-        return remote(spot, spot, zo_send, x_recv.at[edge, ch.index], {"rep": inner})
-
-    def cross(r, ch, send=None):
-        spot = held.at[rows_of(r, fsdp), ch.cols]
-        return remote(spot, spot, x_send if send is None else send, x_recv.at[r, ch.index], {"fsdp": other})
-
-    def crossed(r, ch):
-        spot = held.at[rows_of(r, other), ch.cols]
-        return remote(spot, spot, x_send, x_recv.at[r, ch.index], {"fsdp": other})
-
-    def hop_extra(ch):
-        spot = held.at[rows_of(near, other), ch.cols]
-        return remote(spot, spot, ze_send, x_recv.at[near, ch.index], {"rep": jnp.where(is_edge, near, edge)})
-
-    def all_sent(blocks, width, send):
-        spot = held.at[pl.ds(0, blocks * rows), pl.ds(0, width)]
-        remote(spot, spot, send, gx_recv, {"fsdp": other}).wait_send()
-
-    def among_extra(index):
-        return functools.reduce(jnp.logical_or, [index == at for at in EXTRA])
-
-    def when_extra(ch, act, otherwise):
-        if isinstance(ch.index, int):
-            act() if ch.index in extras else otherwise()
-            return
-        pl.when(among_extra(ch.index))(act)
-        pl.when(jnp.logical_not(among_extra(ch.index)))(otherwise)
-
-    def on_edge(act):
-        pl.when(is_edge)(act)
-
-    def on_middle(act):
-        pl.when(jnp.logical_not(is_edge))(act)
-
-    def chunks_from(low, high, act):
-        if low < min(high, full):
-            @pl.loop(low, min(high, full))
-            def _(index):
-                act(chunk(index))
-        if full < count == high:
-            act(chunk(full))
-
-    grad_across().start()
-    grad_hop(rep, fsdp, True).start()
-    on_middle(lambda: grad_hop(rep, fsdp, False).start())
 
     early = 2
 

time: 98.2 us -> 98.6 us (level)
  no operation moved by 1% of the time
where the time goes in v9:
time: 98.6 us; the launch traced here: 98.5 us
  Pallas kernels  98.5 us (100%)
    pallas_call x1, Pallas kernels, by_kernel(): pl.pallas_call(functools.partial(gather_multiply, entry_count), out_shape...  92.9 us
    pallas_call x1, Pallas kernels, scale(): pl.pallas_call(body, out_shape=jax.ShapeDtypeStruct((half, columns), jnp....  5.58 us

profile of v9, /device:TPU:0, one launch (start us, length us, event | category | flops | bytes accessed | tf_op | source)
XLA Modules:
  0.0 98.5 jit_solution(3205953647068714735)
XLA Ops:
  0.0 92.9 %shard_map.37 = (bf16[2048,3712]{1,0:T(8,128)(2,1)S(1)}, f32[8,128]{1,0:T(8,128)S(1)}) custom-call(bf16[128,3712]{1,0:T(8,128)(2,1)} %gate_ref.1, bf16[128,3712]{1,0:T(8,128)(2,1)} %up_ref.1, bf16[128,4096]{1,0:T(8,128)(2,1)} %grad_ref.1), custom_call_target="tpu_custom_call" | custom-call | tf_op jit(solution)/shard_map/pallas_call | solution.py:614
  92.9 5.6 %shard_map.38 = bf16[2048,3712]{1,0:T(8,128)(2,1)} custom-call(bf16[2048,3712]{1,0:T(8,128)(2,1)S(1)} %get-tuple-element.7.summed_ref, f32[8,128]{1,0:T(8,128)S(1)} %get-tuple-element.8.factor_ref), custom_call_target="tpu_custom_call" | custom-call | tf_op jit(solution)/shard_map/pallas_call | solution.py:675

commit v10 on v9

--- a/solution.py
+++ b/solution.py
@@ -289,7 +289,7 @@
         return jnp.dot(turned[spot, tokens], held[tokens, ch.cols], preferred_element_type=jnp.float32)
 
     def kept(ch):
-        return pl.ds((ch.index - (count - 2)) * WIDTH, ch.size)
+        return pl.ds((ch.index - (count - 3)) * WIDTH, ch.size)
 
     def begin(ch):
         @pl.loop(0, tiles)
@@ -340,25 +340,29 @@
                 with jax.named_scope("multiply"):
                     multiply_tile(lagging, m, squared)
 
-        pl.loop(LAG, count - 2)(step)
+        last_three = [chunk(index) for index in range(count - 3, count)]
+        far_pull, last_pull = events[1:]
+        pl.loop(LAG, count - 3)(step)
         between()
-        ahead, far_pull, last_pull = events
-        last_two = chunk(count - 2), chunk(count - 1)
-        for index, pull in ((count - 2, far_pull), (count - 1, last_pull)):
-            with jax.named_scope("pull_last"):
-                ahead(chunk(index))
-                for ch in last_two:
-                    pull(ch)
-            finish(chunk(index - lag), arrived, squared)
+        with jax.named_scope("far_last"):
+            for ch in last_three:
+                far_pull(ch)
+        remaining = count - 3 - lag
+        chunks_from(remaining, remaining + 1, lambda ch: finish(ch, arrived, squared))
+        with jax.named_scope("pull_last"):
+            last_pull(last_three[0])
+        chunks_from(remaining + 1, count - 3, lambda ch: finish(ch, arrived, squared))
+        with jax.named_scope("pull_last"):
+            for ch in last_three[1:]:
+                last_pull(ch)
         ended()
-        chunks_from(count - lag, count - 2, lambda ch: finish(ch, arrived, squared))
-        for ch in last_two:
+        for ch in last_three:
             with jax.named_scope("begin"):
                 arrived_but_last(ch)
                 begin(ch)
                 if squared:
                     begin_end(ch)
-        for ch in last_two:
+        for ch in last_three:
             with jax.named_scope("late"):
                 crossed(far_edge, ch).wait_recv()
                 complete(ch, squared)
@@ -456,7 +460,7 @@
             grads_sent(2, gz_in)
             all_sent(1, columns, z_in)
             all_sent(1, columns, zo_send)
-            for index in (count - 2, count - 1):
+            for index in range(count - 3, count):
                 begin_end(chunk(index))
 
         sweep([near_ahead, *pulls], arrived, between, lambda: None, EDGE_LAG, False)
@@ -608,7 +612,8 @@
     tokens = rows * n_rep * 2
     half = out_grad.shape[1] // 2
     quarter = half // n_tp
-    count = chunking(columns)[1]
+    full, count, chunk = chunking(columns)
+    kept = 2 * WIDTH + chunk(count - 1).size
     dma = pltpu.SemaphoreType.DMA
     block, whole = dma((n_rep, 2)), dma((n_rep,))
     return pl.pallas_call(
@@ -628,15 +633,15 @@
             pltpu.VMEM((rows, quarter), jnp.bfloat16),
             pltpu.VMEM((2 * n_tp, 8, LANES), jnp.float32),
             pltpu.VMEM((8, LANES), jnp.float32),
-            pltpu.VMEM((half, 2 * WIDTH), jnp.float32),
-            pltpu.VMEM((half, 2 * WIDTH), jnp.float32),
+            pltpu.VMEM((half, kept), jnp.float32),
+            pltpu.VMEM((half, kept), jnp.float32),
             dma((4,)), dma, dma, block, dma, dma, dma, block,
             dma, whole, dma, whole,
             dma((3, count)), dma, dma, dma, dma, dma, dma, dma((n_rep, count)),
             dma, dma, dma, dma,
         ],
         compiler_params=pltpu.CompilerParams(
-            collective_id=0, has_side_effects=True, vmem_limit_bytes=VMEM_LIMIT * 3 // 4
+            collective_id=0, has_side_effects=True, vmem_limit_bytes=VMEM_LIMIT * 4 // 5
         ),
     )(gate_pre, up_pre, out_grad)
 
@@ -698,10 +703,10 @@
 def kernel_fits(n_rep, n_fsdp, n_tp, rows, columns, features):
     tokens, half = rows * n_rep * n_fsdp, features // n_fsdp
     held_bytes = 2 * (tokens * columns + 2 * tokens * half + half * columns + 2 * rows * columns)
-    held_bytes += 16 * half * WIDTH
+    held_bytes += 24 * half * WIDTH
     aligned = rows % 128 == 0 and columns % LANES == 0 and half % (LANES * n_tp) == 0
     shaped = (n_rep, n_fsdp, n_tp) == (4, 2, 4) and columns >= max(12 * WIDTH, 7 * half // n_tp)
-    return shaped and aligned and half % TILE == 0 and held_bytes < VMEM_LIMIT * 3 // 4
+    return shaped and aligned and half % TILE == 0 and held_bytes < VMEM_LIMIT * 4 // 5
 
 
 def solution(mesh):

time: 98.6 us -> 98.5 us (level)
  no operation moved by 1% of the time
where the time goes in v10:
time: 98.5 us; the launch traced here: 98.4 us
  Pallas kernels  98.4 us (100%)
    pallas_call x1, Pallas kernels, by_kernel(): pl.pallas_call(functools.partial(gather_multiply, entry_count), out_shape...  92.8 us
    pallas_call x1, Pallas kernels, scale(): pl.pallas_call(body, out_shape=jax.ShapeDtypeStruct((half, columns), jnp....  5.58 us

profile of v10, /device:TPU:0, one launch (start us, length us, event | category | flops | bytes accessed | tf_op | source)
XLA Modules:
  0.0 98.4 jit_solution(7562414503791216207)
XLA Ops:
  0.0 92.8 %shard_map.37 = (bf16[2048,3712]{1,0:T(8,128)(2,1)S(1)}, f32[8,128]{1,0:T(8,128)S(1)}) custom-call(bf16[128,3712]{1,0:T(8,128)(2,1)} %gate_ref.1, bf16[128,3712]{1,0:T(8,128)(2,1)} %up_ref.1, bf16[128,4096]{1,0:T(8,128)(2,1)} %grad_ref.1), custom_call_target="tpu_custom_call" | custom-call | tf_op jit(solution)/shard_map/pallas_call | solution.py:619
  92.8 5.6 %shard_map.38 = bf16[2048,3712]{1,0:T(8,128)(2,1)} custom-call(bf16[2048,3712]{1,0:T(8,128)(2,1)S(1)} %get-tuple-element.7.summed_ref, f32[8,128]{1,0:T(8,128)S(1)} %get-tuple-element.8.factor_ref), custom_call_target="tpu_custom_call" | custom-call | tf_op jit(solution)/shard_map/pallas_call | solution.py:680

commit v11 on v10

--- a/solution.py
+++ b/solution.py
@@ -11,7 +11,7 @@
 LANES = 128
 VMEM_LIMIT = 60 * 1024 * 1024
 WIDTH = 256
-TILE = 1024
+TILE = 2048
 LAG = 4
 EDGE_LAG = 2
 AHEAD = 4
@@ -344,11 +344,13 @@
         far_pull, last_pull = events[1:]
         pl.loop(LAG, count - 3)(step)
         between()
+        remaining = count - 3 - lag
         with jax.named_scope("far_last"):
-            for ch in last_three:
+            far_pull(last_three[0])
+        chunks_from(remaining, remaining + 1, lambda ch: finish(ch, arrived, squared))
+        with jax.named_scope("far_last"):
+            for ch in last_three[1:]:
                 far_pull(ch)
-        remaining = count - 3 - lag
-        chunks_from(remaining, remaining + 1, lambda ch: finish(ch, arrived, squared))
         with jax.named_scope("pull_last"):
             last_pull(last_three[0])
         chunks_from(remaining + 1, count - 3, lambda ch: finish(ch, arrived, squared))
@@ -460,10 +462,13 @@
             grads_sent(2, gz_in)
             all_sent(1, columns, z_in)
             all_sent(1, columns, zo_send)
-            for index in range(count - 3, count):
-                begin_end(chunk(index))
-
-        sweep([near_ahead, *pulls], arrived, between, lambda: None, EDGE_LAG, False)
+
+        def near_and_part(ch):
+            near_ahead(ch)
+            for at in range(3):
+                pl.when(ch.index == LAG + 2 + at)(lambda: begin_end(chunk(count - 3 + at)))
+
+        sweep([near_and_part, *pulls], arrived, between, lambda: None, EDGE_LAG, False)
         all_sent(1, columns - extra_columns, xn_send)
         all_sent(3, columns, x_send)
 

time: 98.5 us -> 101 us (1.025)
  Pallas kernels: 98.4 us -> 100 us
    pallas_call x1, Pallas kernels: 92.8 us -> 94.8 us  [by_kernel(): pl.pallas_call(functools.partial(gather_multiply, entry_count), out_shape...]
where the time goes in v11:
time: 101 us
  Pallas kernels  100 us (99%)
    pallas_call x1, Pallas kernels, by_kernel(): pl.pallas_call(functools.partial(gather_multiply, entry_count), out_shape...  94.8 us
    pallas_call x1, Pallas kernels, scale(): pl.pallas_call(body, out_shape=jax.ShapeDtypeStruct((half, columns), jnp....  5.58 us

profile of v11, /device:TPU:0, one launch (start us, length us, event | category | flops | bytes accessed | tf_op | source)
XLA Modules:
  0.0 100.6 jit_solution(9025143472713249208)
XLA Ops:
  0.0 94.8 %shard_map.37 = (bf16[2048,3712]{1,0:T(8,128)(2,1)S(1)}, f32[8,128]{1,0:T(8,128)S(1)}) custom-call(bf16[128,3712]{1,0:T(8,128)(2,1)} %gate_ref.1, bf16[128,3712]{1,0:T(8,128)(2,1)} %up_ref.1, bf16[128,4096]{1,0:T(8,128)(2,1)} %grad_ref.1), custom_call_target="tpu_custom_call" | custom-call | tf_op jit(solution)/shard_map/pallas_call | solution.py:624
  94.8 5.6 %shard_map.38 = bf16[2048,3712]{1,0:T(8,128)(2,1)} custom-call(bf16[2048,3712]{1,0:T(8,128)(2,1)S(1)} %get-tuple-element.7.summed_ref, f32[8,128]{1,0:T(8,128)S(1)} %get-tuple-element.8.factor_ref), custom_call_target="tpu_custom_call" | custom-call | tf_op jit(solution)/shard_map/pallas_call | solution.py:685

commit v12 on v11

--- a/solution.py
+++ b/solution.py
@@ -11,7 +11,7 @@
 LANES = 128
 VMEM_LIMIT = 60 * 1024 * 1024
 WIDTH = 256
-TILE = 2048
+TILE = 1024
 LAG = 4
 EDGE_LAG = 2
 AHEAD = 4

time: 101 us -> 98.3 us (0.973)
  Pallas kernels: 100 us -> 98.1 us
    pallas_call x1, Pallas kernels: 94.8 us -> 92.5 us  [by_kernel(): pl.pallas_call(functools.partial(gather_multiply, entry_count), out_shape...]
where the time goes in v12:
time: 98.3 us; the launch traced here: 98.1 us
  Pallas kernels  98.1 us (100%)
    pallas_call x1, Pallas kernels, by_kernel(): pl.pallas_call(functools.partial(gather_multiply, entry_count), out_shape...  92.5 us
    pallas_call x1, Pallas kernels, scale(): pl.pallas_call(body, out_shape=jax.ShapeDtypeStruct((half, columns), jnp....  5.58 us

profile of v12, /device:TPU:0, one launch (start us, length us, event | category | flops | bytes accessed | tf_op | source)
XLA Modules:
  0.0 98.1 jit_solution(6569510043880035348)
XLA Ops:
  0.0 92.5 %shard_map.37 = (bf16[2048,3712]{1,0:T(8,128)(2,1)S(1)}, f32[8,128]{1,0:T(8,128)S(1)}) custom-call(bf16[128,3712]{1,0:T(8,128)(2,1)} %gate_ref.1, bf16[128,3712]{1,0:T(8,128)(2,1)} %up_ref.1, bf16[128,4096]{1,0:T(8,128)(2,1)} %grad_ref.1), custom_call_target="tpu_custom_call" | custom-call | tf_op jit(solution)/shard_map/pallas_call | solution.py:624
  92.6 5.6 %shard_map.38 = bf16[2048,3712]{1,0:T(8,128)(2,1)} custom-call(bf16[2048,3712]{1,0:T(8,128)(2,1)S(1)} %get-tuple-element.7.summed_ref, f32[8,128]{1,0:T(8,128)S(1)} %get-tuple-element.8.factor_ref), custom_call_target="tpu_custom_call" | custom-call | tf_op jit(solution)/shard_map/pallas_call | solution.py:685
